TPU v7x, 8 devices: a whole 2x2x1 slice. The times are simulated.
8 devices in a mesh: part: 1 (over z), loc: 2 (over y), grp: 4 (over x, core).
Axes of the slice: x: 2, y: 2, z: 1, core: 2. Of those that a mesh axis runs over, the one named last changes fastest.
Arguments:
- x_tok: bfloat16 [1024, 1280], P(('part', 'grp', 'loc'))
- expert_ids: int32 [1024, 6], P(('part', 'grp', 'loc'))
- gate_val: float32 [1024, 6], P(('part', 'grp', 'loc'))
- w_gate: bfloat16 [160, 1280, 384], P(('grp', 'loc'))
- w_up: bfloat16 [160, 1280, 384], P(('grp', 'loc'))
- w_down: bfloat16 [160, 384, 1280], P(('grp', 'loc'))
Outputs:
- output: bfloat16 [1024, 1280], P(('part', 'grp', 'loc'))
All inputs are finite; a program needn't handle non-finite values.
Results may differ from a plain program's by a relative error of at most 0.0117378.
Values are sent between devices in bfloat16 or wider.
A program may use at most 1 GiB of HBM per device.

v0:
```python
import jax
import jax.numpy as jnp
from jax import lax
from jax.sharding import PartitionSpec as P


def expert_rows(in_rows, row_ids, row_gate, w_gate, w_up, w_down, first_expert, capacity):
    n_rows, d_model = in_rows.shape
    top_k = row_ids.shape[1]
    n_local = w_gate.shape[0]
    local_ids = (row_ids - first_expert).reshape(-1)
    one_hot = (local_ids[:, None] == jnp.arange(n_local)[None, :]).astype(jnp.int32)
    position = jnp.sum(jnp.cumsum(one_hot, axis=0) * one_hot, axis=1) - 1
    is_valid = jnp.sum(one_hot, axis=1) > 0
    slot_ids = jnp.where(is_valid, local_ids * capacity + position, n_local * capacity)
    src_row = jnp.zeros(n_local * capacity, jnp.int32).at[slot_ids].set(jnp.arange(n_rows * top_k, dtype=jnp.int32) // top_k, mode="drop")
    src_gate = jnp.zeros(n_local * capacity, jnp.float32).at[slot_ids].set(row_gate.reshape(-1), mode="drop")
    packed = jnp.take(in_rows, src_row, axis=0).reshape(n_local, capacity, d_model)
    up_gate = jnp.einsum("ecd,edf->ecf", packed, w_gate, preferred_element_type=jnp.float32)
    up_lin = jnp.einsum("ecd,edf->ecf", packed, w_up, preferred_element_type=jnp.float32)
    hidden = (jax.nn.silu(up_gate) * up_lin).astype(jnp.bfloat16)
    out_rows = jnp.einsum("ecf,efd->ecd", hidden, w_down, preferred_element_type=jnp.float32)
    weighted = out_rows.reshape(n_local * capacity, d_model) * src_gate[:, None]
    return jax.ops.segment_sum(weighted, src_row, num_segments=n_rows)


def solution(mesh):
    n_grp = mesh.shape["grp"]
    n_loc = mesh.shape["loc"]
    tok_spec = P(("part", "grp", "loc"), None)
    w_spec = P(("grp", "loc"), None, None)

    def device_step(x_tok, expert_ids, gate_val, w_gate, w_up, w_down):
        tok_local, d_model = x_tok.shape
        top_k = expert_ids.shape[1]
        n_local = w_gate.shape[0]
        per_group = n_local * n_loc
        tokens_part = tok_local * n_grp * n_loc
        capacity = 8 * (tokens_part * top_k // (4 * per_group * n_grp) + 1)
        first_expert = (lax.axis_index("grp") * n_loc + lax.axis_index("loc")) * n_local
        owner_grp = expert_ids // per_group
        grp_mask = owner_grp[None, :, :] == jnp.arange(n_grp)[:, None, None]
        grp_hit = jnp.any(grp_mask, axis=2)
        send_rows = jnp.where(grp_hit[:, :, None], x_tok[None], jnp.zeros((), x_tok.dtype))
        send_ids = jnp.where(grp_mask, expert_ids[None], -1)
        send_gate = jnp.where(grp_mask, gate_val[None], 0.0)
        n_relay = n_grp * tok_local
        relay_rows = lax.all_to_all(send_rows, "grp", 0, 0, tiled=True).reshape(n_relay, d_model)
        relay_ids = lax.all_to_all(send_ids, "grp", 0, 0, tiled=True).reshape(n_relay, top_k)
        relay_gate = lax.all_to_all(send_gate, "grp", 0, 0, tiled=True).reshape(n_relay, top_k)
        owner_loc = (relay_ids % per_group) // n_local
        loc_mask = (owner_loc[None] == jnp.arange(n_loc)[:, None, None]) & (relay_ids >= 0)[None]
        loc_hit = jnp.any(loc_mask, axis=2)
        fan_rows = jnp.where(loc_hit[:, :, None], relay_rows[None], jnp.zeros((), relay_rows.dtype))
        fan_ids = jnp.where(loc_mask, relay_ids[None], -1)
        fan_gate = jnp.where(loc_mask, relay_gate[None], 0.0)
        got_rows = lax.all_to_all(fan_rows, "loc", 0, 0, tiled=True).reshape(n_loc * n_relay, d_model)
        got_ids = lax.all_to_all(fan_ids, "loc", 0, 0, tiled=True).reshape(n_loc * n_relay, top_k)
        got_gate = lax.all_to_all(fan_gate, "loc", 0, 0, tiled=True).reshape(n_loc * n_relay, top_k)
        row_sums = expert_rows(got_rows, got_ids, got_gate, w_gate, w_up, w_down, first_expert, capacity)
        back_sums = lax.all_to_all(row_sums.reshape(n_loc, n_relay, d_model), "loc", 0, 0, tiled=True)
        group_part = jnp.sum(back_sums, axis=0).astype(jnp.bfloat16).reshape(n_grp, tok_local, d_model)
        home_parts = lax.all_to_all(group_part, "grp", 0, 0, tiled=True)
        return jnp.sum(home_parts, axis=0, dtype=jnp.float32).astype(jnp.bfloat16)

    return jax.shard_map(device_step, mesh=mesh, in_specs=(tok_spec, tok_spec, tok_spec, w_spec, w_spec, w_spec), out_specs=tok_spec, check_vma=False)
```

profile of v0, /device:TPU:0, one launch (start us, length us, event | category | flops | bytes accessed | tf_op | source)
XLA Modules:
  0.0 263.7 jit_solution(7912873856662913711)
XLA Ops:
  0.7 1.3 fusion.19
  2.0 4.6 %all-to-all-start = ((s32[4,128,6]{1,2,0:T(8,128)}), s32[4,128,6]{1,2,0:T(8,128)S(1)}, u32[]{:S(2)}, u32[]{:S(2)}) async-start(s32[4,128,6]{1,2,0:T(8,128)} %fusion.19), calls=%async_computation | async-start | bytes 32768 | tf_op jit(solution)/shard_map/all_to_all | solution.py:49
  7.9 2.2 broadcast_select_fusion.4
  10.3 3.2 %all-to-all-start.4 = ((f32[4,128,6]{1,2,0:T(8,128)}), f32[4,128,6]{1,2,0:T(8,128)S(1)}, u32[]{:S(2)}, u32[]{:S(2)}) async-start(f32[4,128,6]{1,2,0:T(8,128)} %fusion.17), calls=%async_computation.4 | async-start | bytes 32768 | tf_op jit(solution)/shard_map/all_to_all | solution.py:50
  13.6 3.6 %all-to-all-done.4 = f32[4,128,6]{1,2,0:T(8,128)S(1)} async-done(((f32[4,128,6]{1,2,0:T(8,128)}), f32[4,128,6]{1,2,0:T(8,128)S(1)}, u32[]{:S(2)}, u32[]{:S(2)}) %all-to-all-start.4) | async-done | bytes 12320 | tf_op jit(solution)/shard_map/all_to_all | solution.py:50
  18.3 3.3 %all-to-all-start.1 = ((s32[2,512,6]{1,2,0:T(8,128)}), s32[2,512,6]{1,2,0:T(8,128)S(1)}, u32[]{:S(2)}, u32[]{:S(2)}) async-start(s32[2,512,6]{1,2,0:T(8,128)} %fusion.13), calls=%async_computation.1 | async-start | bytes 65536 | tf_op jit(solution)/shard_map/all_to_all | solution.py:58
  21.6 3.7 %all-to-all-done.1 = s32[2,512,6]{1,2,0:T(8,128)S(1)} async-done(((s32[2,512,6]{1,2,0:T(8,128)}), s32[2,512,6]{1,2,0:T(8,128)S(1)}, u32[]{:S(2)}, u32[]{:S(2)}) %all-to-all-start.1) | async-done | bytes 24608 | tf_op jit(solution)/shard_map/all_to_all | solution.py:58
  25.3 3.3 %all-to-all-start.5 = ((f32[2,512,6]{1,2,0:T(8,128)}), f32[2,512,6]{1,2,0:T(8,128)S(1)}, u32[]{:S(2)}, u32[]{:S(2)}) async-start(f32[2,512,6]{1,2,0:T(8,128)} %fusion.11), calls=%async_computation.5 | async-start | bytes 65536 | tf_op jit(solution)/shard_map/all_to_all | solution.py:59
  29.2 3.1 %all-to-all-done.5 = f32[2,512,6]{1,2,0:T(8,128)S(1)} async-done(((f32[2,512,6]{1,2,0:T(8,128)}), f32[2,512,6]{1,2,0:T(8,128)S(1)}, u32[]{:S(2)}, u32[]{:S(2)}) %all-to-all-start.5) | async-done | bytes 24608 | tf_op jit(solution)/shard_map/all_to_all | solution.py:59
  32.3 3.5 %all-to-all-start.2 = ((bf16[4,128,1280]{2,1,0:T(8,128)(2,1)}), bf16[4,128,1280]{2,1,0:T(8,128)(2,1)S(1)}, u32[]{:S(2)}, u32[]{:S(2)}) async-start(bf16[4,128,1280]{2,1,0:T(8,128)(2,1)} %broadcast_select_fusion.4), calls=%async_computation.2 | async-start | bytes 2621440 | tf_op jit(solution)/shard_map/all_to_all | solution.py:48
  37.4 5.9 %reduce-window.6 = s32[20,48,128]{2,1,0:T(8,128)S(1)} reduce-window(s32[20,48,128]{2,1,0:T(8,128)S(1)} %fusion.9, s32[]{:T(128)} %constant.44.clone.1), window={size=1x1x128 pad=0_0x0_0x127_0}, to_apply=%region_1.2 | reduce-window | flops 15605760 | bytes 983044 | tf_op jit(solution)/shard_map/reduce-window
  44.8 8.1 %all-to-all-done.2 = bf16[4,128,1280]{2,1,0:T(8,128)(2,1)S(1)} async-done(((bf16[4,128,1280]{2,1,0:T(8,128)(2,1)}), bf16[4,128,1280]{2,1,0:T(8,128)(2,1)S(1)}, u32[]{:S(2)}, u32[]{:S(2)}) %all-to-all-start.2) | async-done | bytes 1310752 | tf_op jit(solution)/shard_map/all_to_all | solution.py:48
  52.9 1.8 broadcast_select_fusion.3
  54.7 3.9 %all-to-all-start.3 = ((bf16[2,512,1280]{2,1,0:T(8,128)(2,1)}), bf16[2,512,1280]{2,1,0:T(8,128)(2,1)S(1)}, u32[]{:S(2)}, u32[]{:S(2)}) async-start(bf16[2,512,1280]{2,1,0:T(8,128)(2,1)} %broadcast_select_fusion.3), calls=%async_computation.3 | async-start | bytes 5242880 | tf_op jit(solution)/shard_map/all_to_all | solution.py:57
  58.6 23.0 %scatter_custom_fusion = s32[1600]{0:T(1024)S(1)} fusion(s32[6144]{0:T(1024)S(1)} %bitcast.38, s32[6144]{0:T(1024)S(1)} %add_select_fusion, s32[]{:T(128)} %constant.44.clone.1), kind=kCustom, calls=%fused_computation.61 | custom fusion | bytes 6404 | tf_op jit(solution)/shard_map/scatter | solution.py:16
  81.7 23.2 %scatter_custom_fusion.1 = f32[1600]{0:T(1024)S(1)} fusion(s32[6144]{0:T(1024)S(1)} %bitcast.39, f32[6144]{0:T(1024)S(1)} %reshape.162, f32[]{:T(128)} %constant.43.clone.1), kind=kCustom, calls=%fused_computation.57 | custom fusion | bytes 6404 | tf_op jit(solution)/shard_map/scatter | solution.py:17
  104.9 6.8 %gather_fusion = bf16[1600,1280]{1,0:T(8,128)(2,1)} fusion(bf16[1024,1280]{1,0:T(8,128)(2,1)S(1)} %bitcast.26, s32[2048]{0:T(1024)S(1)} %pad_clamp_fusion), kind=kCustom, calls=%fused_computation | custom fusion | bytes 8198400 | tf_op jit(solution)/shard_map/jit(_take)/gather | solution.py:18
  111.6 11.3 %fusion = f32[20,80,384]{2,1,0:T(8,128)S(1)} fusion(bf16[20,1280,384]{2,1,0:T(8,128)(2,1)} %param.10, bf16[20,80,1280]{2,1,0:T(8,128)(2,1)} %bitcast.27, pred[20,80]{1,0:T(8,128)(4,1)S(1)} %broadcast_in_dim.144), kind=kOutput, calls=%fused_computation.6 | convolution fusion | flops 1574912000 | bytes 26216000 | tf_op jit(solution)/shard_map/ecd,edf->ecf/dot_general | solution.py:20
  122.9 20.2 %fusion.6 = f32[20,80,1280]{2,1,0:T(8,128)} fusion(bf16[20,384,1280]{2,1,0:T(8,128)(2,1)} %param.11, f32[20,80,384]{2,1,0:T(8,128)S(1)} %fusion, bf16[20,1280,384]{2,1,0:T(8,128)(2,1)} %param.9, bf16[20,80,1280]{2,1,0:T(8,128)(2,1)} %bitcast.28, pred[20,80]{1,0:T(8,128)(4,1)S(1)} %broadcast_in_dim.144), kind=kOutput, calls=%fused_computation.15 | convolution fusion | flops 3151462400 | bytes 54068800 | tf_op jit(solution)/shard_map/ecf,efd->ecd/dot_general | solution.py:22
  143.1 7.1 %bitcast_multiply_fusion = f32[1600,1280]{1,0:T(8,128)} fusion(f32[20,80,1280]{2,1,0:T(8,128)} %fusion.6, f32[1600]{0:T(1024)S(1)} %scatter_custom_fusion.1), kind=kLoop, calls=%fused_computation.4 | loop fusion | flops 2048000 | bytes 16390400 | tf_op jit(solution)/shard_map/mul | solution.py:23
  150.2 23.0 %scatter_custom_fusion.2 = f32[1024,1280]{1,0:T(8,128)} fusion(s32[1600]{0:T(1024)S(1)} %scatter_custom_fusion, f32[1600,1280]{1,0:T(8,128)} %bitcast_multiply_fusion, f32[]{:T(128)} %constant.43.clone.1), kind=kCustom, calls=%fused_computation.8 | custom fusion | flops 2048000 | bytes 5243392 | tf_op jit(solution)/shard_map/scatter-add | solution.py:24
  173.3 66.7 %all_to_all.40 = f32[2,512,1280]{2,1,0:T(8,128)} all-to-all(f32[2,512,1280]{2,1,0:T(8,128)} %bitcast.29), channel_id=1, replica_groups=mesh['part'=1,'loc'=2,'grp'=4] {'loc'}, dimensions={0} | all-to-all | bytes 10485760 | tf_op jit(solution)/shard_map/all_to_all | solution.py:61
  240.0 3.0 %reduce_sum.41 = bf16[512,1280]{1,0:T(8,128)(2,1)S(1)} reduce(f32[2,512,1280]{2,1,0:T(8,128)} %all_to_all.40, f32[]{:T(128)} %constant.43.clone.1), dimensions={0}, to_apply=%region_9.10 | reduce | flops 655360 | bytes 6553604 | tf_op jit(solution)/shard_map/reduce_sum | solution.py:62
  243.0 19.7 %all_to_all.41 = bf16[4,128,1280]{2,1,0:T(8,128)(2,1)S(1)} all-to-all(bf16[4,128,1280]{2,1,0:T(8,128)(2,1)S(1)} %bitcast.31), channel_id=1, replica_groups=mesh['part'=1,'loc'=2,'grp'=4] {'grp'}, dimensions={0} | all-to-all | bytes 2621440 | tf_op jit(solution)/shard_map/all_to_all | solution.py:63
  (34 shorter events, 8.1 us)
Async XLA Ops:
  2.0 8.3 %all-to-all-start = ((s32[4,128,6]{1,2,0:T(8,128)}), s32[4,128,6]{1,2,0:T(8,128)S(1)}, u32[]{:S(2)}, u32[]{:S(2)}) async-start(s32[4,128,6]{1,2,0:T(8,128)} %fusion.19), calls=%async_computation | async-start | bytes 32768 | tf_op jit(solution)/shard_map/all_to_all | solution.py:49
  10.3 6.9 %all-to-all-start.4 = ((f32[4,128,6]{1,2,0:T(8,128)}), f32[4,128,6]{1,2,0:T(8,128)S(1)}, u32[]{:S(2)}, u32[]{:S(2)}) async-start(f32[4,128,6]{1,2,0:T(8,128)} %fusion.17), calls=%async_computation.4 | async-start | bytes 32768 | tf_op jit(solution)/shard_map/all_to_all | solution.py:50
  18.3 7.0 %all-to-all-start.1 = ((s32[2,512,6]{1,2,0:T(8,128)}), s32[2,512,6]{1,2,0:T(8,128)S(1)}, u32[]{:S(2)}, u32[]{:S(2)}) async-start(s32[2,512,6]{1,2,0:T(8,128)} %fusion.13), calls=%async_computation.1 | async-start | bytes 65536 | tf_op jit(solution)/shard_map/all_to_all | solution.py:58
  25.3 7.0 %all-to-all-start.5 = ((f32[2,512,6]{1,2,0:T(8,128)}), f32[2,512,6]{1,2,0:T(8,128)S(1)}, u32[]{:S(2)}, u32[]{:S(2)}) async-start(f32[2,512,6]{1,2,0:T(8,128)} %fusion.11), calls=%async_computation.5 | async-start | bytes 65536 | tf_op jit(solution)/shard_map/all_to_all | solution.py:59
  32.3 20.5 %all-to-all-start.2 = ((bf16[4,128,1280]{2,1,0:T(8,128)(2,1)}), bf16[4,128,1280]{2,1,0:T(8,128)(2,1)S(1)}, u32[]{:S(2)}, u32[]{:S(2)}) async-start(bf16[4,128,1280]{2,1,0:T(8,128)(2,1)} %broadcast_select_fusion.4), calls=%async_computation.2 | async-start | bytes 2621440 | tf_op jit(solution)/shard_map/all_to_all | solution.py:48
  54.7 50.2 %all-to-all-start.3 = ((bf16[2,512,1280]{2,1,0:T(8,128)(2,1)}), bf16[2,512,1280]{2,1,0:T(8,128)(2,1)S(1)}, u32[]{:S(2)}, u32[]{:S(2)}) async-start(bf16[2,512,1280]{2,1,0:T(8,128)(2,1)} %broadcast_select_fusion.3), calls=%async_computation.3 | async-start | bytes 5242880 | tf_op jit(solution)/shard_map/all_to_all | solution.py:57
where the time goes:
time: 265 us; the launch traced here: 264 us
  blocking collectives  86.4 us (33%)
  local copies, waits for them, and re-layouts  55.9 us (21%)
  other arithmetic  49.4 us (19%)
  matrix products  31.5 us (12%)
  starting transfers between devices  21.8 us (8%)
  waiting for transfers between devices  18.6 us (7%)
    all_to_all x1, blocking collectives, device_step(): lax.all_to_all(row_sums.reshape(n_loc, n_relay, d_model), 'loc', 0, 0, ti...  66.7 us
    scatter x1, local copies, waits for them, and re-layouts, expert_rows(): jnp.zeros(n_local * capacity, jnp.float32).at[slot_ids]  23.2 us
    scatter-add x1, other arithmetic, expert_rows(): return jax.ops.segment_sum(weighted, src_row, num_segments=n_rows)  23 us
    scatter x1, local copies, waits for them, and re-layouts, expert_rows(): jnp.zeros(n_local * capacity, jnp.int32).at[slot_ids]  23 us
    dot_general x1, matrix products, expert_rows(): jnp.einsum('ecf,efd->ecd', hidden, w_down, preferred_element_type=jnp.flo...  20.2 us
    all_to_all x1, blocking collectives, device_step(): home_parts = lax.all_to_all(group_part, 'grp', 0, 0, tiled=True)  19.7 us
    dot_general x1, matrix products, expert_rows(): jnp.einsum('ecd,edf->ecf', packed, w_up, preferred_element_type=jnp.float32)  11.3 us
    all_to_all x1, waiting for transfers between devices, device_step(): lax.all_to_all(send_rows, 'grp', 0, 0, tiled=True).reshape(n_relay, d_model)  8.07 us
  transfers between devices with their start and end apart: 6, of which 5 were waited for; matrix products, arithmetic and copies ran while one was open for 22% of the time, Pallas kernels for 0%

commit v1 on v0

v1 whole, which is shorter than its diff:
```python
import functools

import jax
import jax.numpy as jnp
from jax import lax
from jax.experimental import pallas as pl
from jax.experimental.pallas import tpu as pltpu
from jax.sharding import PartitionSpec as P

F32 = jnp.float32
BF16 = jnp.bfloat16
PACK = 5


def moe_kernel(dims, x_ref, meta_ref, wg_ref, wu_ref, wd_ref, y_ref,
               x_all, meta_all, pos_ref, ge_ref, cols_ref, gate_ref, oh_ref, packed, osp, q_ref,
               s_ref, h_ref, r_ref, gp_ref, parts, wgu, wdn,
               w_sem, xs_sem, xr_sem, ms_sem, mr_sem, ss_sem, rr_sem, gs_sem, pr_sem):
    n_loc, n_grp, n_exp, cap, top_k, n_slot = dims
    tok, d_model = x_ref.shape
    half = tok // 2
    ff = wg_ref.shape[2]
    n_dev = n_loc * n_grp
    n_tok = tok * n_dev
    rows = n_exp * cap
    l = lax.axis_index("loc")
    g = lax.axis_index("grp")
    gx, gc = g // 2, g % 2

    def rel(fx, fc, fl):
        return ((gx + fx) % 2) * 2 + (gc + fc) % 2, (l + fl) % 2

    def dev(fx, fc, fl):
        gg, ll = rel(fx, fc, fl)
        return {"grp": gg, "loc": ll}

    def block_of(fx, fc, fl):
        gg, ll = rel(fx, fc, fl)
        return gg * n_loc + ll

    def weight_copies(e, slot):
        return (
            pltpu.make_async_copy(wg_ref.at[e], wgu.at[slot, :, pl.ds(0, ff)], w_sem.at[slot, 0]),
            pltpu.make_async_copy(wu_ref.at[e], wgu.at[slot, :, pl.ds(ff, ff)], w_sem.at[slot, 1]),
            pltpu.make_async_copy(wd_ref.at[e], wdn.at[slot], w_sem.at[slot, 2]),
        )

    def start_weights(e, carry):
        for copy in weight_copies(e, e):
            copy.start()
        return carry

    lax.fori_loop(0, n_slot, start_weights, 0)

    rels = [(fx, fc, fl) for fx in (0, 1) for fc in (0, 1) for fl in (0, 1)][1:]
    barrier = pltpu.get_barrier_semaphore()
    for r in rels:
        pl.semaphore_signal(barrier, inc=1, device_id=dev(*r), device_id_type=pl.DeviceIdType.MESH)
    pl.semaphore_wait(barrier, len(rels))

    me = block_of(0, 0, 0)
    meta_all[me] = meta_ref[...]
    pending = []

    def send(src, dst, s_sem, r_sem, to):
        copy = pltpu.make_async_remote_copy(
            src_ref=src, dst_ref=dst, send_sem=s_sem, recv_sem=r_sem,
            device_id=dev(*to), device_id_type=pl.DeviceIdType.MESH)
        copy.start()
        pending.append(copy)
        return copy

    metas = [send(meta_ref, meta_all.at[me], ms_sem.at[i], mr_sem.at[i], r) for i, r in enumerate(rels)]

    def x_rows(block, part):
        return x_all.at[pl.ds(pl.multiple_of(block * tok + part * half, half), half), :]

    def r_idx(r):
        return r[0] * 4 + r[1] * 2 + r[2]

    XN, YN, PC, DG = (1, 0, 0), (0, 0, 1), (0, 1, 0), (1, 0, 1)
    n_sent = [0]

    def send_x(src, block, part, to, at):
        i = n_sent[0]
        n_sent[0] += 1
        return send(src, x_rows(block, part), xs_sem.at[i], xr_sem.at[r_idx(at) * 2 + part], to)

    def own(part):
        return x_ref.at[pl.ds(part * half, half), :]

    got = {}
    got[XN, 0] = send_x(own(0), me, 0, XN, XN)
    got[YN, 1] = send_x(own(1), me, 1, YN, YN)
    got[XN, 1] = send_x(own(1), me, 1, XN, XN)
    got[YN, 0] = send_x(own(0), me, 0, YN, YN)
    got[PC, 0] = send_x(own(0), me, 0, PC, PC)
    got[PC, 1] = send_x(own(1), me, 1, PC, PC)
    x_all[pl.ds(pl.multiple_of(me * tok, tok), tok), :] = x_ref[...]

    for copy in metas:
        copy.wait_recv()

    ids_t = jnp.concatenate([meta_all[d, 0:8, :] for d in range(n_dev)], axis=1)
    gts_t = jnp.concatenate([meta_all[d, 8:16, :] for d in range(n_dev)], axis=1)
    e_rows = 32
    e_iota = lax.broadcasted_iota(jnp.int32, (e_rows, n_tok), 0)
    e_ids = jnp.where(e_iota < n_exp, e_iota + me * n_exp, -5).astype(F32)
    mask = jnp.zeros((e_rows, n_tok), F32)
    gate_e = jnp.zeros((e_rows, n_tok), F32)
    for j in range(top_k):
        eq = ids_t[j:j + 1, :] == e_ids
        mask = mask + jnp.where(eq, 1.0, 0.0)
        gate_e = gate_e + jnp.where(eq, gts_t[j:j + 1, :], 0.0)
    blocks = [mask[:, d * tok:(d + 1) * tok] for d in range(n_dev)]
    tri = (lax.broadcasted_iota(jnp.int32, (tok, tok), 0) < lax.broadcasted_iota(jnp.int32, (tok, tok), 1))
    tri = jnp.where(tri, 1.0, 0.0).astype(BF16)
    prefix = jnp.dot(jnp.concatenate(blocks, axis=0).astype(BF16), tri, preferred_element_type=F32)
    offset = jnp.zeros((e_rows, 1), F32)
    pos = []
    for d in range(n_dev):
        pos.append(prefix[d * e_rows:(d + 1) * e_rows, :] + offset)
        offset = offset + jnp.sum(blocks[d], axis=1, keepdims=True)
    pos = jnp.concatenate(pos, axis=1)
    pos_ref[...] = jnp.where(mask > 0.0, pos, -1.0)
    ge_ref[...] = gate_e
    slot_id = e_iota.astype(F32) * float(cap) + pos + 1.0
    slot_rows = [jnp.sum(jnp.where(ids_t[j:j + 1, :] == e_ids, slot_id, 0.0), axis=0, keepdims=True) - 1.0
                 for j in range(top_k)]
    slot_rows += [jnp.full((1, n_tok), -1.0, F32)] * (8 - top_k)
    slot_t = jnp.concatenate(slot_rows, axis=0)
    for d in range(n_dev):
        cols_ref[pl.ds(d * tok, tok), :] = jnp.transpose(slot_t[:, d * tok:(d + 1) * tok])

    def forward(at, part, hops):
        block = block_of(*at)
        for to, seen_as in hops:
            got[seen_as, part] = send_x(x_rows(block, part), block, part, to, seen_as)

    def landed(at, part):
        got[at, part].wait_recv()

    PX, PY, PD = (1, 1, 0), (0, 1, 1), (1, 1, 1)
    landed(XN, 0)
    forward(XN, 0, [(YN, DG), (PC, PX)])
    landed(YN, 1)
    forward(YN, 1, [(XN, DG), (PC, PY)])
    landed(XN, 1)
    forward(XN, 1, [(PC, PX)])
    landed(YN, 0)
    forward(YN, 0, [(PC, PY)])
    landed(DG, 0)
    forward(DG, 0, [(PC, PD)])
    landed(DG, 1)
    forward(DG, 1, [(PC, PD)])
    for at in (PC, PX, PY, PD):
        for part in (0, 1):
            landed(at, part)

    step = 256

    def pack(p, carry):
        for i in range(PACK):
            e = p * PACK + i
            where = lax.broadcasted_iota(jnp.int32, (cap, n_tok), 0).astype(F32) == pos_ref[pl.ds(e, 1), :]
            oh_ref[pl.ds(i * cap, cap), :] = jnp.where(where, 1.0, 0.0).astype(BF16)
            gate_ref[pl.ds(pl.multiple_of(e * cap, 16), cap), :] = jnp.sum(
                jnp.where(where, ge_ref[pl.ds(e, 1), :], 0.0), axis=1, keepdims=True)
        base = pl.multiple_of(p * (PACK * cap), 16)
        for n in range(d_model // step):
            cols = pl.ds(n * step, step)
            packed[pl.ds(base, PACK * cap), cols] = jnp.dot(
                oh_ref[...], x_all[:, cols], preferred_element_type=F32).astype(BF16)
        return carry

    lax.fori_loop(0, n_exp // PACK, pack, 0)

    def expert(e, carry):
        slot = e % n_slot
        for copy in weight_copies(e, slot):
            copy.wait()
        at = pl.ds(pl.multiple_of(e * cap, 16), cap)
        uv = jnp.dot(packed[at, :], wgu[slot], preferred_element_type=F32)
        hid = (jax.nn.silu(uv[:, :ff]) * uv[:, ff:]).astype(BF16)
        out = jnp.dot(hid, wdn[slot], preferred_element_type=F32) * gate_ref[at, :]
        hi = out.astype(BF16)
        rest = out - hi.astype(F32)
        mid = rest.astype(BF16)
        osp[0, at, :] = hi
        osp[1, at, :] = mid
        osp[2, at, :] = (rest - mid.astype(F32)).astype(BF16)

        @pl.when(e + n_slot < n_exp)
        def _():
            for copy in weight_copies(e + n_slot, slot):
                copy.start()
        return carry

    lax.fori_loop(0, n_exp, expert, 0)

    def combine(block, dst):
        cols = cols_ref[pl.ds(pl.multiple_of(block * tok, tok), tok), :]
        lanes = lax.broadcasted_iota(jnp.int32, (tok, rows), 1).astype(F32)
        hit = cols[:, 0:1] == lanes
        for j in range(1, top_k):
            hit = hit | (cols[:, j:j + 1] == lanes)
        q_ref[...] = jnp.where(hit, 1.0, 0.0).astype(BF16)
        for n in range(d_model // step):
            at = pl.ds(n * step, step)
            total = jnp.dot(q_ref[...], osp[0, :, at], preferred_element_type=F32)
            total += jnp.dot(q_ref[...], osp[1, :, at], preferred_element_type=F32)
            total += jnp.dot(q_ref[...], osp[2, :, at], preferred_element_type=F32)
            dst[:, at] = total

    def home_grp(k):
        fx = 1 - k // 2
        fc = ((k + 1) // 2) % 2
        return ((gx + fx) % 2) * 2 + (gc + fc) % 2

    def y_copy(k):
        return pltpu.make_async_remote_copy(
            src_ref=s_ref.at[k], dst_ref=r_ref.at[k], send_sem=ss_sem.at[k], recv_sem=rr_sem.at[k],
            device_id=dev(*YN), device_id_type=pl.DeviceIdType.MESH)

    def away(k, carry):
        combine(home_grp(k) * n_loc + (1 - l), s_ref.at[k])
        y_copy(k).start()
        return carry

    def home(k, carry):
        combine(home_grp(k) * n_loc + l, h_ref.at[k])
        return carry

    lax.fori_loop(0, n_grp, away, 0)
    lax.fori_loop(0, n_grp, home, 0)

    flips = [(1, 0, 0), (1, 1, 0), (0, 1, 0)]
    returns = []
    for k in range(n_grp):
        y_copy(k).wait_recv()
        part = (h_ref[k] + r_ref[k]).astype(BF16)
        if k < 3:
            gp_ref[k] = part
            returns.append(send(gp_ref.at[k], parts.at[k], gs_sem.at[k], pr_sem.at[k], flips[k]))
        else:
            parts[k] = part
    for copy in returns:
        copy.wait_recv()
    total = parts[0].astype(F32)
    for k in range(1, n_grp):
        total = total + parts[k].astype(F32)
    y_ref[...] = total.astype(BF16)
    for copy in pending:
        copy.wait_send()
    for k in range(n_grp):
        y_copy(k).wait_send()


def solution(mesh):
    n_grp = mesh.shape["grp"]
    n_loc = mesh.shape["loc"]
    tok_spec = P(("part", "grp", "loc"), None)
    w_spec = P(("grp", "loc"), None, None)

    def device_step(x_tok, expert_ids, gate_val, w_gate, w_up, w_down):
        tok, d_model = x_tok.shape
        top_k = expert_ids.shape[1]
        n_exp, _, ff = w_gate.shape
        n_dev = n_grp * n_loc
        n_tok = tok * n_dev
        cap = 8 * (n_tok * top_k // (4 * n_exp * n_dev) + 1)
        rows = n_exp * cap
        n_slot = 9
        meta = jnp.zeros((16, tok), F32)
        meta = meta.at[0:top_k].set(expert_ids.T.astype(F32)).at[8:8 + top_k].set(gate_val.T)
        vmem = pltpu.VMEM
        dma = pltpu.SemaphoreType.DMA
        dims = (n_loc, n_grp, n_exp, cap, top_k, n_slot)
        return pl.pallas_call(
            functools.partial(moe_kernel, dims),
            out_shape=jax.ShapeDtypeStruct((tok, d_model), BF16),
            in_specs=[pl.BlockSpec(memory_space=vmem)] * 2 + [pl.BlockSpec(memory_space=pl.ANY)] * 3,
            out_specs=pl.BlockSpec(memory_space=vmem),
            scratch_shapes=[
                vmem((n_tok, d_model), BF16),
                vmem((n_dev, 16, tok), F32),
                vmem((32, n_tok), F32),
                vmem((32, n_tok), F32),
                vmem((n_tok, 8), F32),
                vmem((rows, 1), F32),
                vmem((PACK * cap, n_tok), BF16),
                vmem((rows, d_model), BF16),
                vmem((3, rows, d_model), BF16),
                vmem((tok, rows), BF16),
                vmem((n_grp, tok, d_model), F32),
                vmem((n_grp, tok, d_model), F32),
                vmem((n_grp, tok, d_model), F32),
                vmem((n_grp, tok, d_model), BF16),
                vmem((n_grp, tok, d_model), BF16),
                vmem((n_slot, d_model, 2 * ff), BF16),
                vmem((n_slot, ff, d_model), BF16),
                dma((n_slot, 3)),
                dma((14,)),
                dma((16,)),
                dma((7,)),
                dma((7,)),
                dma((n_grp,)),
                dma((n_grp,)),
                dma((n_grp,)),
                dma((n_grp,)),
            ],
            compiler_params=pltpu.CompilerParams(
                collective_id=0, has_side_effects=True, vmem_limit_bytes=67043328),
            name="moe",
        )(x_tok, meta, w_gate, w_up, w_down)

    return jax.shard_map(device_step, mesh=mesh, in_specs=(tok_spec, tok_spec, tok_spec, w_spec, w_spec, w_spec), out_specs=tok_spec, check_vma=False)
```

time: 265 us -> 109 us (0.41)
  Pallas kernels: 0 us -> 105 us
  blocking collectives: 86.4 us -> 0 us
  local copies, waits for them, and re-layouts: 55.9 us -> 3.63 us
  other arithmetic: 49.4 us -> 0.69 us
  matrix products: 31.5 us -> 0 us
  starting transfers between devices: 21.8 us -> 0 us
  waiting for transfers between devices: 18.6 us -> 0 us
    pallas_call x0 -> x1, Pallas kernels: none -> 105 us  [device_step(): pl.pallas_call(functools.partial(moe_kernel, dims), out_shape=jax.ShapeDt...]
    all_to_all x2 -> x0, blocking collectives: 86.4 us -> none  [the longest x1 66.7 us: device_step(): lax.all_to_all(row_sums.reshape(n_loc, n_relay, d_model), 'loc', 0, 0, ti...]
    scatter x2, local copies, waits for them, and re-layouts: 46.1 us -> 1.91 us  [device_step(): meta.at[0:top_k].set(expert_ids.T.astype(F32)).at[8:8 + top_k]]
    dot_general x2 -> x0, matrix products: 31.5 us -> none  [the longest x1 20.2 us: expert_rows(): jnp.einsum('ecf,efd->ecd', hidden, w_down, preferred_element_type=jnp.flo...]
    scatter-add x1 -> x0, other arithmetic: 23 us -> none  [expert_rows(): return jax.ops.segment_sum(weighted, src_row, num_segments=n_rows)]
    all_to_all x6 -> x0, starting transfers between devices: 21.8 us -> none  [the longest x1 4.61 us: device_step(): lax.all_to_all(send_ids, 'grp', 0, 0, tiled=True).reshape(n_relay, top_k)]
    all_to_all x6 -> x0, waiting for transfers between devices: 18.6 us -> none  [the longest x1 8.07 us: device_step(): lax.all_to_all(send_rows, 'grp', 0, 0, tiled=True).reshape(n_relay, d_model)]
    select_n x11 -> x0, other arithmetic: 8.6 us -> none  [the longest x1 2.2 us: device_step(): jnp.where(grp_hit[:, :, None], x_tok[None], jnp.zeros((), x_tok.dtype))]
  transfers between devices with their start and end apart: 6 -> 0, of which waited for: 5 -> 0; matrix products, arithmetic and copies ran while one was open for 22% -> 0% of each run, Pallas kernels for 0% -> 0%
where the time goes in v1:
time: 109 us
  Pallas kernels  105 us (96%)
  local copies, waits for them, and re-layouts  3.63 us (3%)
    pallas_call x1, Pallas kernels, device_step(): pl.pallas_call(functools.partial(moe_kernel, dims), out_shape=jax.ShapeDt...  105 us

profile of v1, /device:TPU:0, one launch (start us, length us, event | category | flops | bytes accessed | tf_op | source)
XLA Modules:
  0.0 109.0 jit_solution(6568113060741188073)
XLA Ops:
  0.0 0.7 convert_bitcast_fusion
  0.7 0.6 scatter.6
  1.3 1.3 %scatter.9.meta_ref = f32[16,128]{1,0:T(8,128)} dynamic-update-slice(f32[16,128]{1,0:T(8,128)} %scatter.6, f32[6,128]{1,0:T(8,128)} %bitcast.3, s32[]{:T(128)} %constant.55.clone.1, s32[]{:T(128)} %constant.56.clone.1) | dynamic-update-slice | bytes 6148 | tf_op jit(solution)/shard_map/scatter | solution.py:275
  2.6 104.7 %moe.1 = bf16[128,1280]{1,0:T(8,128)(2,1)} custom-call(bf16[128,1280]{1,0:T(8,128)(2,1)} %x_ref.1, f32[16,128]{1,0:T(8,128)} %scatter.9.meta_ref, bf16[20,1280,384]{2,1,0:T(8,128)(2,1)} %wg_ref.1, bf16[20,1280,384]{2,1,0:T(8,128)(2,1)} %wu_ref.1, bf16[20,384,1280]{2,1,0:T(8,128)(2,1)} %wd_ref.1), custom_call_target="tpu_custom_call" | custom-call | tf_op jit(solution)/shard_map/moe/pallas_call | solution.py:279
  107.3 1.7 %copy.9 = bf16[128,1280]{1,0:T(8,128)(2,1)} copy(bf16[128,1280]{1,0:T(8,128)(2,1)} %moe.1) | data formatting | bytes 655360

commit v2 on v1

v2 whole, which is shorter than its diff:
```python
import functools

import jax
import jax.numpy as jnp
from jax import lax
from jax.experimental import pallas as pl
from jax.experimental.pallas import tpu as pltpu
from jax.sharding import PartitionSpec as P

F32 = jnp.float32
BF16 = jnp.bfloat16
PACK = 5


YN, YP, DG, DP = (0, 0, 1), (0, 1, 1), (1, 0, 1), (1, 1, 1)
XN, XP, ME, PC = (1, 0, 0), (1, 1, 0), (0, 0, 0), (0, 1, 0)
ORDER = [YN, YP, DG, DP, XN, XP, ME, PC]


def flip(a, b):
    return tuple((i + j) % 2 for i, j in zip(a, b))


def moe_kernel(dims, x_ref, meta_ref, wg_ref, wu_ref, wd_ref, y_ref,
               x_all, meta_all, pos_ref, ge_ref, cols_ref, gate_ref, oh_ref, packed, osp, q_ref,
               c_ref, d_ref, rf_ref, rs_ref, gp_ref, gx_ref, wgu, wdn,
               w_sem, xs_sem, xr_sem, ms_sem, mr_sem, ds_sem, dr_sem, ts_sem, tr_sem):
    n_loc, n_grp, n_exp, cap, top_k, n_slot = dims
    tok, d_model = x_ref.shape
    half = tok // 2
    ff = wg_ref.shape[2]
    n_dev = n_loc * n_grp
    n_tok = tok * n_dev
    rows = n_exp * cap
    l = lax.axis_index("loc")
    g = lax.axis_index("grp")
    gx, gc = g // 2, g % 2

    def dev(to):
        fx, fc, fl = to
        return {"grp": ((gx + fx) % 2) * 2 + (gc + fc) % 2, "loc": (l + fl) % 2}

    def weight_copies(e, slot):
        return (
            pltpu.make_async_copy(wg_ref.at[e], wgu.at[slot, :, pl.ds(0, ff)], w_sem.at[slot, 0]),
            pltpu.make_async_copy(wu_ref.at[e], wgu.at[slot, :, pl.ds(ff, ff)], w_sem.at[slot, 1]),
            pltpu.make_async_copy(wd_ref.at[e], wdn.at[slot], w_sem.at[slot, 2]),
        )

    def start_weights(e, carry):
        for copy in weight_copies(e, e):
            copy.start()
        return carry

    lax.fori_loop(0, n_slot, start_weights, 0)

    peers = [r for r in ORDER if r != ME]
    barrier = pltpu.get_barrier_semaphore()
    for r in peers:
        pl.semaphore_signal(barrier, inc=1, device_id=dev(r), device_id_type=pl.DeviceIdType.MESH)
    pl.semaphore_wait(barrier, len(peers))

    pending = []

    def send(src, dst, s_sem, r_sem, to):
        copy = pltpu.make_async_remote_copy(
            src_ref=src, dst_ref=dst, send_sem=s_sem, recv_sem=r_sem,
            device_id=dev(to), device_id_type=pl.DeviceIdType.MESH)
        copy.start()
        pending.append(copy)
        return copy

    metas = [send(meta_ref, meta_all.at[ORDER.index(r)], ms_sem.at[i], mr_sem.at[i], r) for i, r in enumerate(peers)]

    def x_rows(at, part):
        return x_all.at[pl.ds(ORDER.index(at) * tok + part * half, half), :]

    got = {}

    def send_x(src, part, to, at):
        i = len(got)
        got[at, part] = send(src, x_rows(at, part), xs_sem.at[i], xr_sem.at[ORDER.index(at) * 2 + part], to)

    for part, to in ((0, XN), (1, YN), (1, XN), (0, YN), (0, PC), (1, PC)):
        send_x(x_ref.at[pl.ds(part * half, half), :], part, to, to)
    x_all[pl.ds(ORDER.index(ME) * tok, tok), :] = x_ref[...]
    meta_all[ORDER.index(ME)] = meta_ref[...]

    for copy in metas:
        copy.wait_recv()

    ids_t = jnp.concatenate([meta_all[d, 0:8, :] for d in range(n_dev)], axis=1)
    gts_t = jnp.concatenate([meta_all[d, 8:16, :] for d in range(n_dev)], axis=1)
    e_rows = 32
    e_iota = lax.broadcasted_iota(jnp.int32, (e_rows, n_tok), 0)
    e_ids = jnp.where(e_iota < n_exp, e_iota + (g * n_loc + l) * n_exp, -5).astype(F32)
    mask = jnp.zeros((e_rows, n_tok), F32)
    gate_e = jnp.zeros((e_rows, n_tok), F32)
    for j in range(top_k):
        eq = ids_t[j:j + 1, :] == e_ids
        mask = mask + jnp.where(eq, 1.0, 0.0)
        gate_e = gate_e + jnp.where(eq, gts_t[j:j + 1, :], 0.0)
    blocks = [mask[:, d * tok:(d + 1) * tok] for d in range(n_dev)]
    tri = (lax.broadcasted_iota(jnp.int32, (tok, tok), 0) < lax.broadcasted_iota(jnp.int32, (tok, tok), 1))
    tri = jnp.where(tri, 1.0, 0.0).astype(BF16)
    prefix = jnp.dot(jnp.concatenate(blocks, axis=0).astype(BF16), tri, preferred_element_type=F32)
    offset = jnp.zeros((e_rows, 1), F32)
    pos = []
    for d in range(n_dev):
        pos.append(prefix[d * e_rows:(d + 1) * e_rows, :] + offset)
        offset = offset + jnp.sum(blocks[d], axis=1, keepdims=True)
    pos = jnp.concatenate(pos, axis=1)
    pos_ref[...] = jnp.where(mask > 0.0, pos, -1.0)
    ge_ref[...] = gate_e
    slot_id = e_iota.astype(F32) * float(cap) + pos + 1.0
    slot_rows = [jnp.sum(jnp.where(ids_t[j:j + 1, :] == e_ids, slot_id, 0.0), axis=0, keepdims=True) - 1.0
                 for j in range(top_k)]

    def group_hit(grp):
        low = (lax.broadcasted_iota(jnp.int32, (1, n_tok), 1) * 0 + grp * (n_loc * n_exp)).astype(F32)
        hit = jnp.zeros((1, n_tok), F32)
        for j in range(top_k):
            inside = (ids_t[j:j + 1, :] >= low) & (ids_t[j:j + 1, :] < low + float(n_loc * n_exp))
            hit = jnp.where(inside, 1.0, hit)
        return hit

    own_hit = group_hit(g)
    slot_rows += [own_hit, own_hit * group_hit(gx * 2 + (gc + 1) % 2)]
    slot_t = jnp.concatenate(slot_rows, axis=0)
    for d in range(n_dev):
        cols_ref[pl.ds(d * tok, tok), :] = jnp.transpose(slot_t[:, d * tok:(d + 1) * tok])

    def forward(at, part, hops):
        for to in hops:
            send_x(x_rows(at, part), part, to, flip(at, to))

    def landed(at, part):
        got[at, part].wait_recv()

    landed(XN, 0)
    forward(XN, 0, [YN, PC])
    landed(YN, 1)
    forward(YN, 1, [XN, PC])
    landed(XN, 1)
    forward(XN, 1, [PC])
    landed(YN, 0)
    forward(YN, 0, [PC])
    landed(YP, 0)
    landed(YP, 1)

    step = 256

    def run_pass(number, first, count):
        toks = pl.ds(first, count)

        def pack(p, carry):
            for i in range(PACK):
                e = p * PACK + i
                where = lax.broadcasted_iota(jnp.int32, (cap, count), 0).astype(F32) == pos_ref[pl.ds(e, 1), toks]
                oh_ref[pl.ds(i * cap, cap), pl.ds(0, count)] = jnp.where(where, 1.0, 0.0).astype(BF16)
                gate_ref[pl.ds(pl.multiple_of(e * cap, 16), cap), :] = jnp.sum(
                    jnp.where(where, ge_ref[pl.ds(e, 1), toks], 0.0), axis=1, keepdims=True)
            base = pl.multiple_of(p * (PACK * cap), 16)
            for n in range(d_model // step):
                cols = pl.ds(n * step, step)
                packed[pl.ds(base, PACK * cap), cols] = jnp.dot(
                    oh_ref[:, pl.ds(0, count)], x_all[toks, cols], preferred_element_type=F32).astype(BF16)
            return carry

        lax.fori_loop(0, n_exp // PACK, pack, 0)

        def expert(e, carry):
            turn = e + number * n_exp
            slot = turn % n_slot
            for copy in weight_copies(e, slot):
                copy.wait()
            at = pl.ds(pl.multiple_of(e * cap, 16), cap)
            uv = jnp.dot(packed[at, :], wgu[slot], preferred_element_type=F32)
            hid = (jax.nn.silu(uv[:, :ff]) * uv[:, ff:]).astype(BF16)
            out = jnp.dot(hid, wdn[slot], preferred_element_type=F32) * gate_ref[at, :]
            hi = out.astype(BF16)
            rest = out - hi.astype(F32)
            mid = rest.astype(BF16)
            osp[0, at, :] = hi
            osp[1, at, :] = mid
            osp[2, at, :] = (rest - mid.astype(F32)).astype(BF16)

            @pl.when(turn + n_slot < 2 * n_exp)
            def _():
                for copy in weight_copies((turn + n_slot) % n_exp, slot):
                    copy.start()
            return carry

        lax.fori_loop(0, n_exp, expert, 0)

    def combine(blk):
        cols = cols_ref[pl.ds(pl.multiple_of(blk * tok, tok), tok), :]
        lanes = lax.broadcasted_iota(jnp.int32, (tok, rows), 1).astype(F32)
        hit = cols[:, 0:1] == lanes
        for j in range(1, top_k):
            hit = hit | (cols[:, j:j + 1] == lanes)
        q_ref[...] = jnp.where(hit, 1.0, 0.0).astype(BF16)
        for n in range(d_model // step):
            at = pl.ds(n * step, step)
            total = jnp.dot(q_ref[...], osp[0, :, at], preferred_element_type=F32)
            total += jnp.dot(q_ref[...], osp[1, :, at], preferred_element_type=F32)
            total += jnp.dot(q_ref[...], osp[2, :, at], preferred_element_type=F32)
            c_ref[blk, :, at] = total

    def swap_copy(h):
        return pltpu.make_async_remote_copy(
            src_ref=c_ref.at[2 * h + 1], dst_ref=d_ref.at[h], send_sem=ds_sem.at[h], recv_sem=dr_sem.at[h],
            device_id=dev(PC), device_id_type=pl.DeviceIdType.MESH)

    def combine_loop(count, pick):
        def body(i, carry):
            blk = pick(i)
            combine(blk)

            @pl.when(blk % 2 == 1)
            def _():
                swap_copy(blk // 2).start()
            return carry

        lax.fori_loop(0, count, body, 0)

    def split_rows(h):
        swap_copy(h).wait_recv()
        cols = cols_ref[pl.ds(2 * h * tok, tok), :]
        mine = c_ref[2 * h]
        other = d_ref[h]
        c_ref[2 * h] = jnp.where(cols[:, 6:7] > 0.5, mine, other)
        d_ref[h] = jnp.where(cols[:, 7:8] > 0.5, other, 0.0)

    def ship(i, src, dst, to):
        return send(src, dst, ts_sem.at[i], tr_sem.at[i], to)

    run_pass(0, 0, 2 * tok)
    landed(DG, 0)
    forward(DG, 0, [PC])
    landed(DG, 1)
    forward(DG, 1, [PC])
    combine_loop(2, lambda i: 1 - i)
    split_rows(0)
    first_own = ship(0, c_ref.at[0], rf_ref.at[0], YN)

    for at in (XP, PC, DP):
        landed(at, 0)
        landed(at, 1)
    run_pass(1, 2 * tok, n_tok - 2 * tok)
    combine_loop(2, lambda i: 3 - i)
    split_rows(1)
    first_far = ship(1, c_ref.at[2], rf_ref.at[1], YN)
    hop = ship(2, d_ref.at[1], rs_ref.at[0], XN)
    combine_loop(4, lambda i: 5 + 2 * i - (i // 2) * 5)
    hop.wait_recv()
    d_ref[0] = d_ref[0] + rs_ref[0]
    second = ship(3, d_ref.at[0], rs_ref.at[1], YN)
    split_rows(2)
    far_second = ship(4, d_ref.at[2], rs_ref.at[2], XN)
    split_rows(3)

    first_own.wait_recv()
    total = (c_ref[6] + rf_ref[0]).astype(BF16).astype(F32)
    c_ref[6] = total
    first_far.wait_recv()
    gp_ref[...] = (c_ref[4] + rf_ref[1]).astype(BF16)
    far_first = ship(5, gp_ref, gx_ref, XN)
    far_second.wait_recv()
    d_ref[3] = d_ref[3] + rs_ref[2]
    far_first.wait_recv()
    c_ref[6] = c_ref[6] + gx_ref[...].astype(F32)
    second.wait_recv()
    y_ref[...] = (c_ref[6] + (d_ref[3] + rs_ref[1]).astype(BF16).astype(F32)).astype(BF16)
    for copy in pending:
        copy.wait_send()
    for h in range(n_dev // 2):
        swap_copy(h).wait_send()


def solution(mesh):
    n_grp = mesh.shape["grp"]
    n_loc = mesh.shape["loc"]
    tok_spec = P(("part", "grp", "loc"), None)
    w_spec = P(("grp", "loc"), None, None)

    def device_step(x_tok, expert_ids, gate_val, w_gate, w_up, w_down):
        tok, d_model = x_tok.shape
        top_k = expert_ids.shape[1]
        n_exp, _, ff = w_gate.shape
        n_dev = n_grp * n_loc
        n_tok = tok * n_dev
        cap = 8 * (n_tok * top_k // (4 * n_exp * n_dev) + 1)
        rows = n_exp * cap
        n_slot = 9
        blank = jnp.zeros((tok, 8 - top_k), F32)
        meta = jnp.concatenate([expert_ids.astype(F32), blank, gate_val, blank], axis=1).T
        vmem = pltpu.VMEM
        dma = pltpu.SemaphoreType.DMA
        dims = (n_loc, n_grp, n_exp, cap, top_k, n_slot)
        return pl.pallas_call(
            functools.partial(moe_kernel, dims),
            out_shape=jax.ShapeDtypeStruct((tok, d_model), BF16),
            in_specs=[pl.BlockSpec(memory_space=vmem)] * 2 + [pl.BlockSpec(memory_space=pl.ANY)] * 3,
            out_specs=pl.BlockSpec(memory_space=vmem),
            scratch_shapes=[
                vmem((n_tok, d_model), BF16),
                vmem((n_dev, 16, tok), F32),
                vmem((32, n_tok), F32),
                vmem((32, n_tok), F32),
                vmem((n_tok, 8), F32),
                vmem((rows, 1), F32),
                vmem((PACK * cap, n_tok - 2 * tok), BF16),
                vmem((rows, d_model), BF16),
                vmem((3, rows, d_model), BF16),
                vmem((tok, rows), BF16),
                vmem((n_dev, tok, d_model), F32),
                vmem((n_dev // 2, tok, d_model), F32),
                vmem((2, tok, d_model), F32),
                vmem((3, tok, d_model), F32),
                vmem((tok, d_model), BF16),
                vmem((tok, d_model), BF16),
                vmem((n_slot, d_model, 2 * ff), BF16),
                vmem((n_slot, ff, d_model), BF16),
                dma((n_slot, 3)),
                dma((14,)),
                dma((16,)),
                dma((7,)),
                dma((7,)),
                dma((n_dev // 2,)),
                dma((n_dev // 2,)),
                dma((6,)),
                dma((6,)),
            ],
            compiler_params=pltpu.CompilerParams(
                collective_id=0, has_side_effects=True, vmem_limit_bytes=67043328),
            name="moe",
        )(x_tok, meta, w_gate, w_up, w_down)

    return jax.shard_map(device_step, mesh=mesh, in_specs=(tok_spec, tok_spec, tok_spec, w_spec, w_spec, w_spec), out_specs=tok_spec, check_vma=False)
```

time: 109 us -> 112 us (1.028)
  Pallas kernels: 105 us -> 108 us
  local copies, waits for them, and re-layouts: 3.63 us -> 1.72 us
  other arithmetic: 0.69 us -> 1.98 us
    pallas_call x1, Pallas kernels: 105 us -> 108 us  [device_step(): pl.pallas_call(functools.partial(moe_kernel, dims), out_shape=jax.ShapeDt...]
    scatter x2 -> x0, local copies, waits for them, and re-layouts: 1.91 us -> none  [device_step(): meta.at[0:top_k].set(expert_ids.T.astype(F32)).at[8:8 + top_k]]
    transpose x0 -> x1, other arithmetic: none -> 1.29 us  [device_step(): jnp.concatenate([expert_ids.astype(F32), blank, gate_val, blank], axis=1)]
where the time goes in v2:
time: 112 us
  Pallas kernels  108 us (96%)
  other arithmetic  1.98 us (2%)
  local copies, waits for them, and re-layouts  1.72 us (2%)
    pallas_call x1, Pallas kernels, device_step(): pl.pallas_call(functools.partial(moe_kernel, dims), out_shape=jax.ShapeDt...  108 us

profile of v2, /device:TPU:0, one launch (start us, length us, event | category | flops | bytes accessed | tf_op | source)
XLA Modules:
  0.0 111.8 jit_solution(4698942096075954199)
XLA Ops:
  0.0 0.7 convert_element_type.3
  0.7 1.3 %maximum_bitcast_fusion.meta_ref = f32[16,128]{1,0:T(8,128)} fusion(f32[128,2]{0,1:T(2,128)S(1)} %broadcast_in_dim.3, f32[128,6]{0,1:T(8,128)} %param.8, f32[128,6]{0,1:T(8,128)S(1)} %convert_element_type.3), kind=kLoop, calls=%fused_computation | loop fusion | flops 6144 | bytes 15360 | tf_op jit(solution)/shard_map/transpose | solution.py:297
  2.0 108.1 %moe.1 = bf16[128,1280]{1,0:T(8,128)(2,1)} custom-call(bf16[128,1280]{1,0:T(8,128)(2,1)} %x_ref.1, f32[16,128]{1,0:T(8,128)} %maximum_bitcast_fusion.meta_ref, bf16[20,1280,384]{2,1,0:T(8,128)(2,1)} %wg_ref.1, bf16[20,1280,384]{2,1,0:T(8,128)(2,1)} %wu_ref.1, bf16[20,384,1280]{2,1,0:T(8,128)(2,1)} %wd_ref.1), custom_call_target="tpu_custom_call" | custom-call | tf_op jit(solution)/shard_map/moe/pallas_call | solution.py:301
  110.1 1.7 %copy.8 = bf16[128,1280]{1,0:T(8,128)(2,1)} copy(bf16[128,1280]{1,0:T(8,128)(2,1)} %moe.1) | data formatting | bytes 655360
  (1 shorter events, 0.0 us)

commit v3 on v2

--- a/solution.py
+++ b/solution.py
@@ -10,6 +10,7 @@
 F32 = jnp.float32
 BF16 = jnp.bfloat16
 PACK = 5
+PAIR = 2
 
 
 YN, YP, DG, DP = (0, 0, 1), (0, 1, 1), (1, 0, 1), (1, 1, 1)
@@ -21,8 +22,8 @@
     return tuple((i + j) % 2 for i, j in zip(a, b))
 
 
-def moe_kernel(dims, x_ref, meta_ref, wg_ref, wu_ref, wd_ref, y_ref,
-               x_all, meta_all, pos_ref, ge_ref, cols_ref, gate_ref, oh_ref, packed, osp, q_ref,
+def moe_kernel(dims, x_ref, ids_ref, gates_ref, wg_ref, wu_ref, wd_ref, y_ref,
+               x_all, ids_all, gates_all, pos_ref, ge_ref, cols_ref, gate_ref, oh_ref, packed, hid_ref, osp, q_ref,
                c_ref, d_ref, rf_ref, rs_ref, gp_ref, gx_ref, wgu, wdn,
                w_sem, xs_sem, xr_sem, ms_sem, mr_sem, ds_sem, dr_sem, ts_sem, tr_sem):
     n_loc, n_grp, n_exp, cap, top_k, n_slot = dims
@@ -40,16 +41,19 @@
         fx, fc, fl = to
         return {"grp": ((gx + fx) % 2) * 2 + (gc + fc) % 2, "loc": (l + fl) % 2}
 
-    def weight_copies(e, slot):
+    def in_copies(e, slot):
         return (
             pltpu.make_async_copy(wg_ref.at[e], wgu.at[slot, :, pl.ds(0, ff)], w_sem.at[slot, 0]),
             pltpu.make_async_copy(wu_ref.at[e], wgu.at[slot, :, pl.ds(ff, ff)], w_sem.at[slot, 1]),
-            pltpu.make_async_copy(wd_ref.at[e], wdn.at[slot], w_sem.at[slot, 2]),
         )
 
+    def out_copy(e, slot):
+        return pltpu.make_async_copy(wd_ref.at[e], wdn.at[slot], w_sem.at[slot, 2])
+
     def start_weights(e, carry):
-        for copy in weight_copies(e, e):
+        for copy in in_copies(e, e):
             copy.start()
+        out_copy(e, e).start()
         return carry
 
     lax.fori_loop(0, n_slot, start_weights, 0)
@@ -70,7 +74,10 @@
         pending.append(copy)
         return copy
 
-    metas = [send(meta_ref, meta_all.at[ORDER.index(r)], ms_sem.at[i], mr_sem.at[i], r) for i, r in enumerate(peers)]
+    metas = []
+    for i, r in enumerate(peers):
+        for k, (src, dst) in enumerate(((ids_ref, ids_all), (gates_ref, gates_all))):
+            metas.append(send(src, dst.at[ORDER.index(r)], ms_sem.at[i, k], mr_sem.at[i, k], r))
 
     def x_rows(at, part):
         return x_all.at[pl.ds(ORDER.index(at) * tok + part * half, half), :]
@@ -84,13 +91,14 @@
     for part, to in ((0, XN), (1, YN), (1, XN), (0, YN), (0, PC), (1, PC)):
         send_x(x_ref.at[pl.ds(part * half, half), :], part, to, to)
     x_all[pl.ds(ORDER.index(ME) * tok, tok), :] = x_ref[...]
-    meta_all[ORDER.index(ME)] = meta_ref[...]
+    ids_all[ORDER.index(ME)] = ids_ref[...]
+    gates_all[ORDER.index(ME)] = gates_ref[...]
 
     for copy in metas:
         copy.wait_recv()
 
-    ids_t = jnp.concatenate([meta_all[d, 0:8, :] for d in range(n_dev)], axis=1)
-    gts_t = jnp.concatenate([meta_all[d, 8:16, :] for d in range(n_dev)], axis=1)
+    ids_t = jnp.concatenate([ids_all[d] for d in range(n_dev)], axis=1).astype(F32)
+    gts_t = jnp.concatenate([gates_all[d] for d in range(n_dev)], axis=1)
     e_rows = 32
     e_iota = lax.broadcasted_iota(jnp.int32, (e_rows, n_tok), 0)
     e_ids = jnp.where(e_iota < n_exp, e_iota + (g * n_loc + l) * n_exp, -5).astype(F32)
@@ -150,7 +158,7 @@
 
     step = 256
 
-    def run_pass(number, first, count):
+    def run_pass(first, count):
         toks = pl.ds(first, count)
 
         def pack(p, carry):
@@ -169,15 +177,17 @@
 
         lax.fori_loop(0, n_exp // PACK, pack, 0)
 
-        def expert(e, carry):
-            turn = e + number * n_exp
-            slot = turn % n_slot
-            for copy in weight_copies(e, slot):
-                copy.wait()
+        def ring(ref_copies, e):
+            return ref_copies(e, e % n_slot)
+
+        def first_dot(e, i):
             at = pl.ds(pl.multiple_of(e * cap, 16), cap)
-            uv = jnp.dot(packed[at, :], wgu[slot], preferred_element_type=F32)
-            hid = (jax.nn.silu(uv[:, :ff]) * uv[:, ff:]).astype(BF16)
-            out = jnp.dot(hid, wdn[slot], preferred_element_type=F32) * gate_ref[at, :]
+            uv = jnp.dot(packed[at, :], wgu[e % n_slot], preferred_element_type=F32)
+            return (jax.nn.silu(uv[:, :ff]) * uv[:, ff:]).astype(BF16)
+
+        def second_dot(hid, e):
+            at = pl.ds(pl.multiple_of(e * cap, 16), cap)
+            out = jnp.dot(hid, wdn[e % n_slot], preferred_element_type=F32) * gate_ref[at, :]
             hi = out.astype(BF16)
             rest = out - hi.astype(F32)
             mid = rest.astype(BF16)
@@ -185,13 +195,45 @@
             osp[1, at, :] = mid
             osp[2, at, :] = (rest - mid.astype(F32)).astype(BF16)
 
-            @pl.when(turn + n_slot < 2 * n_exp)
-            def _():
-                for copy in weight_copies((turn + n_slot) % n_exp, slot):
+        def wait_in(e):
+            for copy in ring(in_copies, e):
+                copy.wait()
+
+        for i in range(PAIR):
+            wait_in(i)
+        for i in range(PAIR):
+            hid_ref[i] = first_dot(i, i)
+
+        def experts(p, carry):
+            now = [p * PAIR + i for i in range(PAIR)]
+            for e in now:
+                wait_in(e + PAIR)
+                ring(out_copy, e).wait()
+            held = [hid_ref[i] for i in range(PAIR)]
+            for i, e in enumerate(now):
+                hid_ref[i] = first_dot(e + PAIR, i)
+                second_dot(held[i], e)
+
+            for e in now:
+                @pl.when(e + PAIR + n_slot < n_exp)
+                def _():
+                    for copy in in_copies(e + PAIR + n_slot, (e + PAIR) % n_slot):
+                        copy.start()
+
+                @pl.when(e + n_slot < n_exp)
+                def _():
+                    out_copy(e + n_slot, e % n_slot).start()
+            return carry
+
+        for i in range(PAIR):
+            if i + n_slot < n_exp:
+                for copy in in_copies(i + n_slot, i):
                     copy.start()
-            return carry
-
-        lax.fori_loop(0, n_exp, expert, 0)
+        lax.fori_loop(0, n_exp // PAIR - 1, experts, 0)
+        for i in range(PAIR):
+            ring(out_copy, n_exp - PAIR + i).wait()
+        for i in range(PAIR):
+            second_dot(hid_ref[i], n_exp - PAIR + i)
 
     def combine(blk):
         cols = cols_ref[pl.ds(pl.multiple_of(blk * tok, tok), tok), :]
@@ -235,19 +277,17 @@
     def ship(i, src, dst, to):
         return send(src, dst, ts_sem.at[i], tr_sem.at[i], to)
 
-    run_pass(0, 0, 2 * tok)
     landed(DG, 0)
     forward(DG, 0, [PC])
     landed(DG, 1)
     forward(DG, 1, [PC])
+    for at in (XP, PC, DP):
+        landed(at, 0)
+        landed(at, 1)
+    run_pass(0, n_tok)
     combine_loop(2, lambda i: 1 - i)
     split_rows(0)
     first_own = ship(0, c_ref.at[0], rf_ref.at[0], YN)
-
-    for at in (XP, PC, DP):
-        landed(at, 0)
-        landed(at, 1)
-    run_pass(1, 2 * tok, n_tok - 2 * tok)
     combine_loop(2, lambda i: 3 - i)
     split_rows(1)
     first_far = ship(1, c_ref.at[2], rf_ref.at[1], YN)
@@ -293,25 +333,25 @@
         cap = 8 * (n_tok * top_k // (4 * n_exp * n_dev) + 1)
         rows = n_exp * cap
         n_slot = 9
-        blank = jnp.zeros((tok, 8 - top_k), F32)
-        meta = jnp.concatenate([expert_ids.astype(F32), blank, gate_val, blank], axis=1).T
         vmem = pltpu.VMEM
         dma = pltpu.SemaphoreType.DMA
         dims = (n_loc, n_grp, n_exp, cap, top_k, n_slot)
         return pl.pallas_call(
             functools.partial(moe_kernel, dims),
             out_shape=jax.ShapeDtypeStruct((tok, d_model), BF16),
-            in_specs=[pl.BlockSpec(memory_space=vmem)] * 2 + [pl.BlockSpec(memory_space=pl.ANY)] * 3,
+            in_specs=[pl.BlockSpec(memory_space=vmem)] * 3 + [pl.BlockSpec(memory_space=pl.ANY)] * 3,
             out_specs=pl.BlockSpec(memory_space=vmem),
             scratch_shapes=[
                 vmem((n_tok, d_model), BF16),
-                vmem((n_dev, 16, tok), F32),
+                vmem((n_dev, top_k, tok), jnp.int32),
+                vmem((n_dev, top_k, tok), F32),
                 vmem((32, n_tok), F32),
                 vmem((32, n_tok), F32),
                 vmem((n_tok, 8), F32),
                 vmem((rows, 1), F32),
-                vmem((PACK * cap, n_tok - 2 * tok), BF16),
+                vmem((PACK * cap, n_tok), BF16),
                 vmem((rows, d_model), BF16),
+                vmem((PAIR, cap, ff), BF16),
                 vmem((3, rows, d_model), BF16),
                 vmem((tok, rows), BF16),
                 vmem((n_dev, tok, d_model), F32),
@@ -325,8 +365,8 @@
                 dma((n_slot, 3)),
                 dma((14,)),
                 dma((16,)),
-                dma((7,)),
-                dma((7,)),
+                dma((7, 2)),
+                dma((7, 2)),
                 dma((n_dev // 2,)),
                 dma((n_dev // 2,)),
                 dma((6,)),
@@ -335,6 +375,6 @@
             compiler_params=pltpu.CompilerParams(
                 collective_id=0, has_side_effects=True, vmem_limit_bytes=67043328),
             name="moe",
-        )(x_tok, meta, w_gate, w_up, w_down)
+        )(x_tok, expert_ids.T, gate_val.T, w_gate, w_up, w_down)
 
     return jax.shard_map(device_step, mesh=mesh, in_specs=(tok_spec, tok_spec, tok_spec, w_spec, w_spec, w_spec), out_specs=tok_spec, check_vma=False)

time: 112 us -> 89.7 us (0.80)
  Pallas kernels: 108 us -> 87.8 us
  other arithmetic: 1.98 us -> 0 us
    pallas_call x1, Pallas kernels: 108 us -> 87.8 us  [device_step(): pl.pallas_call(functools.partial(moe_kernel, dims), out_shape=jax.ShapeDt...]
    transpose x1 -> x0, other arithmetic: 1.29 us -> none  [device_step(): jnp.concatenate([expert_ids.astype(F32), blank, gate_val, blank], axis=1)]
where the time goes in v3:
time: 89.7 us; the launch traced here: 89.5 us
  Pallas kernels  87.8 us (98%)
  local copies, waits for them, and re-layouts  1.72 us (2%)
    pallas_call x1, Pallas kernels, device_step(): pl.pallas_call(functools.partial(moe_kernel, dims), out_shape=jax.ShapeDt...  87.8 us

profile of v3, /device:TPU:0, one launch (start us, length us, event | category | flops | bytes accessed | tf_op | source)
XLA Modules:
  0.0 89.5 jit_solution(648588977385604670)
XLA Ops:
  0.0 87.8 %moe.1 = bf16[128,1280]{1,0:T(8,128)(2,1)} custom-call(bf16[128,1280]{1,0:T(8,128)(2,1)} %x_ref.1, s32[6,128]{1,0:T(8,128)} %bitcast.2, f32[6,128]{1,0:T(8,128)} %bitcast.3, bf16[20,1280,384]{2,1,0:T(8,128)(2,1)} %wg_ref.1, bf16[20,1280,384]{2,1,0:T(8,128)(2,1)} %wu_ref.1, bf16[20,384,1280]{2,1,0:T(8,128)(2,1)} %wd_ref.1), custom_call_target="tpu_custom_call" | custom-call | tf_op jit(solution)/shard_map/moe/pallas_call | solution.py:339
  87.8 1.7 %copy.8 = bf16[128,1280]{1,0:T(8,128)(2,1)} copy(bf16[128,1280]{1,0:T(8,128)(2,1)} %moe.1) | data formatting | bytes 655360

commit v4 on v3

v4 whole, which is shorter than its diff:
```python
import functools

import jax
import jax.numpy as jnp
from jax import lax
from jax.experimental import pallas as pl
from jax.experimental.pallas import tpu as pltpu
from jax.sharding import PartitionSpec as P

F32 = jnp.float32
BF16 = jnp.bfloat16
PACK = 5
PAIR = 2


YN, YP, DG, DP = (0, 0, 1), (0, 1, 1), (1, 0, 1), (1, 1, 1)
XN, XP, ME, PC = (1, 0, 0), (1, 1, 0), (0, 0, 0), (0, 1, 0)
ORDER = [YN, YP, XN, XP, ME, PC, DG, DP]


def flip(a, b):
    return tuple((i + j) % 2 for i, j in zip(a, b))


def moe_kernel(dims, x_ref, ids_ref, gates_ref, wg_ref, wu_ref, wd_ref, y_ref,
               x_all, ids_all, gates_all, pos_ref, ge_ref, cols_ref, gate_ref, oh_ref, packed, hid_ref, osp, q_ref, qp_ref, qn_ref,
               c_ref, d_ref, rf_ref, rs_ref, gp_ref, gx_ref, wgu, wdn,
               in_sem, w_sem, xs_sem, xr_sem, ms_sem, mr_sem, ds_sem, dr_sem, ts_sem, tr_sem, ns_sem, nr_sem):
    n_loc, n_grp, n_exp, cap, top_k, n_slot = dims
    tok, d_model = x_ref.shape
    half = tok // 2
    own = ORDER.index(ME)
    ff = wg_ref.shape[2]
    n_dev = n_loc * n_grp
    n_tok = tok * n_dev
    rows = n_exp * cap
    l = lax.axis_index("loc")
    g = lax.axis_index("grp")
    gx, gc = g // 2, g % 2

    def dev(to):
        fx, fc, fl = to
        return {"grp": ((gx + fx) % 2) * 2 + (gc + fc) % 2, "loc": (l + fl) % 2}

    def in_copies(e, slot):
        return (
            pltpu.make_async_copy(wg_ref.at[e], wgu.at[slot, :, pl.ds(0, ff)], w_sem.at[slot, 0]),
            pltpu.make_async_copy(wu_ref.at[e], wgu.at[slot, :, pl.ds(ff, ff)], w_sem.at[slot, 1]),
        )

    def out_copy(e, slot):
        return pltpu.make_async_copy(wd_ref.at[e], wdn.at[slot], w_sem.at[slot, 2])

    def start_weights(e, carry):
        for copy in in_copies(e, e):
            copy.start()
        out_copy(e, e).start()
        return carry

    loads = [
        pltpu.make_async_copy(src, dst, in_sem.at[i]) for i, (src, dst) in enumerate((
            (x_ref, x_all.at[pl.ds(own * tok, tok), :]), (ids_ref, ids_all.at[own]), (gates_ref, gates_all.at[own])))]
    for copy in loads:
        copy.start()

    peers = [r for r in ORDER if r != ME]
    barrier = pltpu.get_barrier_semaphore()
    for r in peers:
        pl.semaphore_signal(barrier, inc=1, device_id=dev(r), device_id_type=pl.DeviceIdType.MESH)
    lax.fori_loop(0, n_slot, start_weights, 0)
    pl.semaphore_wait(barrier, len(peers))
    for copy in loads:
        copy.wait()

    pending = []

    class Sent:
        def __init__(self, *described):
            self.described = described
            self.copy().start()
            pending.append(self)

        def copy(self):
            src, dst, s_sem, r_sem, to = self.described
            return pltpu.make_async_remote_copy(
                src_ref=src(), dst_ref=dst(), send_sem=s_sem(), recv_sem=r_sem(),
                device_id=dev(to), device_id_type=pl.DeviceIdType.MESH)

        def wait_recv(self):
            self.copy().wait_recv()

        def wait_send(self):
            self.copy().wait_send()

    def send(src, dst, s_sem, r_sem, to):
        return Sent(lambda: src, lambda: dst, lambda: s_sem, lambda: r_sem, to)

    metas = []
    for i, r in enumerate(peers):
        for k, (src, dst) in enumerate(((ids_all.at[own], ids_all), (gates_all.at[own], gates_all))):
            metas.append(send(src, dst.at[ORDER.index(r)], ms_sem.at[i, k], mr_sem.at[i, k], r))

    def x_rows(at, part):
        return x_all.at[pl.ds(ORDER.index(at) * tok + part * half, half), :]

    got = {}

    def send_x(src, part, to, at):
        i = len(got)
        got[at, part] = Sent(lambda: x_rows(*src), lambda: x_rows(at, part), lambda: xs_sem.at[i],
                             lambda: xr_sem.at[ORDER.index(at) * 2 + part], to)

    for part, to in ((0, XN), (1, YN), (1, XN), (0, YN), (0, PC), (1, PC)):
        send_x((ME, part), part, to, to)

    for copy in metas:
        copy.wait_recv()

    ids_t = jnp.concatenate([ids_all[d] for d in range(n_dev)], axis=1).astype(F32)
    gts_t = jnp.concatenate([gates_all[d] for d in range(n_dev)], axis=1)
    e_rows = 32
    e_iota = lax.broadcasted_iota(jnp.int32, (e_rows, n_tok), 0)
    e_ids = jnp.where(e_iota < n_exp, e_iota + (g * n_loc + l) * n_exp, -5).astype(F32)
    mask = jnp.zeros((e_rows, n_tok), F32)
    gate_e = jnp.zeros((e_rows, n_tok), F32)
    for j in range(top_k):
        eq = ids_t[j:j + 1, :] == e_ids
        mask = mask + jnp.where(eq, 1.0, 0.0)
        gate_e = gate_e + jnp.where(eq, gts_t[j:j + 1, :], 0.0)
    blocks = [mask[:, d * tok:(d + 1) * tok] for d in range(n_dev)]
    tri = (lax.broadcasted_iota(jnp.int32, (tok, tok), 0) < lax.broadcasted_iota(jnp.int32, (tok, tok), 1))
    tri = jnp.where(tri, 1.0, 0.0).astype(BF16)
    prefix = jnp.dot(jnp.concatenate(blocks, axis=0).astype(BF16), tri, preferred_element_type=F32)
    offset = jnp.zeros((e_rows, 1), F32)
    pos = []
    for d in range(n_dev):
        pos.append(prefix[d * e_rows:(d + 1) * e_rows, :] + offset)
        offset = offset + jnp.sum(blocks[d], axis=1, keepdims=True)
    pos = jnp.concatenate(pos, axis=1)
    pos_ref[...] = jnp.where(mask > 0.0, pos, -1.0)
    ge_ref[...] = gate_e
    slot_id = e_iota.astype(F32) * float(cap) + pos + 1.0
    slot_rows = [jnp.sum(jnp.where(ids_t[j:j + 1, :] == e_ids, slot_id, 0.0), axis=0, keepdims=True) - 1.0
                 for j in range(top_k)]

    def group_hit(grp):
        low = (lax.broadcasted_iota(jnp.int32, (1, n_tok), 1) * 0 + grp * (n_loc * n_exp)).astype(F32)
        hit = jnp.zeros((1, n_tok), F32)
        for j in range(top_k):
            inside = (ids_t[j:j + 1, :] >= low) & (ids_t[j:j + 1, :] < low + float(n_loc * n_exp))
            hit = jnp.where(inside, 1.0, hit)
        return hit

    own_hit = group_hit(g)
    slot_rows += [own_hit, own_hit * group_hit(gx * 2 + (gc + 1) % 2)]
    slot_t = jnp.concatenate(slot_rows, axis=0)
    for d in range(n_dev):
        cols_ref[pl.ds(d * tok, tok), :] = jnp.transpose(slot_t[:, d * tok:(d + 1) * tok])

    def selection(blk):
        cols = cols_ref[pl.ds(blk * tok, tok), :]
        lanes = lax.broadcasted_iota(jnp.int32, (tok, rows), 1).astype(F32)
        hit = cols[:, 0:1] == lanes
        for j in range(1, top_k):
            hit = hit | (cols[:, j:j + 1] == lanes)
        return jnp.where(hit, 1.0, 0.0).astype(BF16)

    qp_ref[...] = selection(ORDER.index(YP))
    qn_ref[...] = selection(ORDER.index(YN))

    def forward(at, part, hops):
        for to in hops:
            send_x((at, part), part, to, flip(at, to))

    def landed(at, part):
        got[at, part].wait_recv()

    landed(XN, 0)
    forward(XN, 0, [YN, PC])
    landed(YN, 1)
    forward(YN, 1, [XN, PC])
    landed(XN, 1)
    forward(XN, 1, [PC])
    landed(YN, 0)
    forward(YN, 0, [PC])
    landed(YP, 0)
    landed(YP, 1)

    step = 256

    def pack(first, count, add, midway):
        toks = pl.ds(first, count)

        def body(p, carry):
            for i in range(PACK):
                e = p * PACK + i
                where = lax.broadcasted_iota(jnp.int32, (cap, count), 0).astype(F32) == pos_ref[pl.ds(e, 1), toks]
                oh_ref[pl.ds(i * cap, cap), pl.ds(0, count)] = jnp.where(where, 1.0, 0.0).astype(BF16)
                gate = jnp.sum(jnp.where(where, ge_ref[pl.ds(e, 1), toks], 0.0), axis=1, keepdims=True)
                at = pl.ds(pl.multiple_of(e * cap, 16), cap)
                gate_ref[at, :] = gate_ref[at, :] + gate if add else gate
            at = pl.ds(pl.multiple_of(p * (PACK * cap), 16), PACK * cap)
            for n in range(d_model // step):
                cols = pl.ds(n * step, step)
                part = jnp.dot(oh_ref[:, pl.ds(0, count)], x_all[toks, cols], preferred_element_type=F32)
                if add:
                    part = part + packed[at, cols].astype(F32)
                packed[at, cols] = part.astype(BF16)
            if midway is not None:
                @pl.when(p == 1)
                def _():
                    midway()
            return carry

        lax.fori_loop(0, n_exp // PACK, body, 0)

    def diagonal():
        for part in (0, 1):
            landed(DG, part)
            forward(DG, part, [PC])

    for at in (XP, PC):
        landed(at, 0)
        landed(at, 1)
    pack(0, n_tok - 2 * tok, False, diagonal)
    landed(DP, 0)
    landed(DP, 1)
    pack(n_tok - 2 * tok, 2 * tok, True, None)

    def ring(ref_copies, e):
        return ref_copies(e, e % n_slot)

    def first_dot(e, i):
        at = pl.ds(pl.multiple_of(e * cap, 16), cap)
        uv = jnp.dot(packed[at, :], wgu[e % n_slot], preferred_element_type=F32)
        return (jax.nn.silu(uv[:, :ff]) * uv[:, ff:]).astype(BF16)

    def second_dot(hid, e):
        at = pl.ds(pl.multiple_of(e * cap, 16), cap)
        out = jnp.dot(hid, wdn[e % n_slot], preferred_element_type=F32) * gate_ref[at, :]
        hi = out.astype(BF16)
        rest = out - hi.astype(F32)
        mid = rest.astype(BF16)
        osp[0, at, :] = hi
        osp[1, at, :] = mid
        osp[2, at, :] = (rest - mid.astype(F32)).astype(BF16)

    def wait_in(e):
        for copy in ring(in_copies, e):
            copy.wait()

    for i in range(PAIR):
        wait_in(i)
    for i in range(PAIR):
        hid_ref[i] = first_dot(i, i)

    def experts(p, carry):
        now = [p * PAIR + i for i in range(PAIR)]
        for e in now:
            wait_in(e + PAIR)
            ring(out_copy, e).wait()
        held = [hid_ref[i] for i in range(PAIR)]
        for i, e in enumerate(now):
            hid_ref[i] = first_dot(e + PAIR, i)
            second_dot(held[i], e)

        for e in now:
            @pl.when(e + PAIR + n_slot < n_exp)
            def _():
                for copy in in_copies(e + PAIR + n_slot, (e + PAIR) % n_slot):
                    copy.start()

            @pl.when(e + n_slot < n_exp)
            def _():
                out_copy(e + n_slot, e % n_slot).start()
        return carry

    for i in range(PAIR):
        if i + n_slot < n_exp:
            for copy in in_copies(i + n_slot, i):
                copy.start()
    lax.fori_loop(0, n_exp // PAIR - 1, experts, 0)
    for i in range(PAIR):
        ring(out_copy, n_exp - PAIR + i).wait()
    for i in range(PAIR):
        second_dot(hid_ref[i], n_exp - PAIR + i)

    def combine(q, blk, chunks):
        for n in chunks:
            at = pl.ds(n * step, step)
            total = jnp.dot(q[...], osp[0, :, at], preferred_element_type=F32)
            total += jnp.dot(q[...], osp[1, :, at], preferred_element_type=F32)
            total += jnp.dot(q[...], osp[2, :, at], preferred_element_type=F32)
            c_ref[blk, :, at] = total

    def swap_copy(h):
        return pltpu.make_async_remote_copy(
            src_ref=c_ref.at[2 * h + 1], dst_ref=d_ref.at[h], send_sem=ds_sem.at[h], recv_sem=dr_sem.at[h],
            device_id=dev(PC), device_id_type=pl.DeviceIdType.MESH)

    def combine_loop(count, pick):
        def body(i, carry):
            blk = pick(i)
            q_ref[...] = selection(pl.multiple_of(blk, 1))
            combine(q_ref, blk, range(d_model // step))

            @pl.when(blk % 2 == 1)
            def _():
                swap_copy(blk // 2).start()
            return carry

        lax.fori_loop(0, count, body, 0)

    everything = pl.ds(0, d_model)

    def split_rows(h, at):
        cols = cols_ref[pl.ds(2 * h * tok, tok), :]
        mine = c_ref[2 * h, :, at]
        other = d_ref[h, :, at]
        c_ref[2 * h, :, at] = jnp.where(cols[:, 6:7] > 0.5, mine, other)
        d_ref[h, :, at] = jnp.where(cols[:, 7:8] > 0.5, other, 0.0)

    def ship(i, src, dst, to):
        return send(src, dst, ts_sem.at[i], tr_sem.at[i], to)

    first_own = []
    for i, chunks in enumerate((range(0, 2), range(2, d_model // step))):
        at = pl.ds(chunks[0] * step, len(chunks) * step)
        combine(qp_ref, ORDER.index(YP), chunks)
        swap = send(c_ref.at[ORDER.index(YP), :, at], d_ref.at[0, :, at], ns_sem.at[i], nr_sem.at[i], PC)
        combine(qn_ref, ORDER.index(YN), chunks)
        swap.wait_recv()
        split_rows(0, at)
        first_own.append(send(c_ref.at[0, :, at], rf_ref.at[0, :, at], ns_sem.at[2 + i], nr_sem.at[2 + i], YN))
    combine_loop(2, lambda i: 7 - i)
    swap_copy(3).wait_recv()
    split_rows(3, everything)
    first_far = ship(1, c_ref.at[6], rf_ref.at[1], YN)
    hop = ship(2, d_ref.at[3], rs_ref.at[0], XN)
    combine_loop(4, lambda i: 3 + 2 * i - (i // 2) * 5)
    hop.wait_recv()
    d_ref[0] = d_ref[0] + rs_ref[0]
    second = ship(3, d_ref.at[0], rs_ref.at[1], YN)
    for h in (1, 2):
        swap_copy(h).wait_recv()
        split_rows(h, everything)
        if h == 1:
            far_second = ship(4, d_ref.at[1], rs_ref.at[2], XN)

    for copy in first_own:
        copy.wait_recv()
    c_ref[4] = (c_ref[4] + rf_ref[0]).astype(BF16).astype(F32)
    first_far.wait_recv()
    gp_ref[...] = (c_ref[2] + rf_ref[1]).astype(BF16)
    far_first = ship(5, gp_ref, gx_ref, XN)
    far_second.wait_recv()
    d_ref[2] = d_ref[2] + rs_ref[2]
    far_first.wait_recv()
    c_ref[4] = c_ref[4] + gx_ref[...].astype(F32)
    second.wait_recv()
    y_ref[...] = (c_ref[4] + (d_ref[2] + rs_ref[1]).astype(BF16).astype(F32)).astype(BF16)
    for copy in pending:
        copy.wait_send()
    for h in range(1, n_dev // 2):
        swap_copy(h).wait_send()


def solution(mesh):
    n_grp = mesh.shape["grp"]
    n_loc = mesh.shape["loc"]
    tok_spec = P(("part", "grp", "loc"), None)
    w_spec = P(("grp", "loc"), None, None)

    def device_step(x_tok, expert_ids, gate_val, w_gate, w_up, w_down):
        tok, d_model = x_tok.shape
        top_k = expert_ids.shape[1]
        n_exp, _, ff = w_gate.shape
        n_dev = n_grp * n_loc
        n_tok = tok * n_dev
        cap = 8 * (n_tok * top_k // (4 * n_exp * n_dev) + 1)
        rows = n_exp * cap
        n_slot = 9
        vmem = pltpu.VMEM
        dma = pltpu.SemaphoreType.DMA
        dims = (n_loc, n_grp, n_exp, cap, top_k, n_slot)
        return pl.pallas_call(
            functools.partial(moe_kernel, dims),
            out_shape=jax.ShapeDtypeStruct((tok, d_model), BF16),
            in_specs=[pl.BlockSpec(memory_space=pl.ANY)] * 6,
            out_specs=pl.BlockSpec(memory_space=vmem),
            scratch_shapes=[
                vmem((n_tok, d_model), BF16),
                vmem((n_dev, top_k, tok), jnp.int32),
                vmem((n_dev, top_k, tok), F32),
                vmem((32, n_tok), F32),
                vmem((32, n_tok), F32),
                vmem((n_tok, 8), F32),
                vmem((rows, 1), F32),
                vmem((PACK * cap, n_tok), BF16),
                vmem((rows, d_model), BF16),
                vmem((PAIR, cap, ff), BF16),
                vmem((3, rows, d_model), BF16),
                vmem((tok, rows), BF16),
                vmem((tok, rows), BF16),
                vmem((tok, rows), BF16),
                vmem((n_dev, tok, d_model), F32),
                vmem((n_dev // 2, tok, d_model), F32),
                vmem((2, tok, d_model), F32),
                vmem((3, tok, d_model), F32),
                vmem((tok, d_model), BF16),
                vmem((tok, d_model), BF16),
                vmem((n_slot, d_model, 2 * ff), BF16),
                vmem((n_slot, ff, d_model), BF16),
                dma((3,)),
                dma((n_slot, 3)),
                dma((14,)),
                dma((16,)),
                dma((7, 2)),
                dma((7, 2)),
                dma((n_dev // 2,)),
                dma((n_dev // 2,)),
                dma((6,)),
                dma((6,)),
                dma((4,)),
                dma((4,)),
            ],
            compiler_params=pltpu.CompilerParams(
                collective_id=0, has_side_effects=True, vmem_limit_bytes=67043328),
            name="moe",
        )(x_tok, expert_ids.T, gate_val.T, w_gate, w_up, w_down)

    return jax.shard_map(device_step, mesh=mesh, in_specs=(tok_spec, tok_spec, tok_spec, w_spec, w_spec, w_spec), out_specs=tok_spec, check_vma=False)
```

time: 89.7 us -> 86.5 us (0.964)
  Pallas kernels: 87.8 us -> 84.6 us
    pallas_call x1, Pallas kernels: 87.8 us -> 84.6 us  [device_step(): pl.pallas_call(functools.partial(moe_kernel, dims), out_shape=jax.ShapeDt...]
where the time goes in v4:
time: 86.5 us; the launch traced here: 86.3 us
  Pallas kernels  84.6 us (98%)
  local copies, waits for them, and re-layouts  1.72 us (2%)
    pallas_call x1, Pallas kernels, device_step(): pl.pallas_call(functools.partial(moe_kernel, dims), out_shape=jax.ShapeDt...  84.6 us

profile of v4, /device:TPU:0, one launch (start us, length us, event | category | flops | bytes accessed | tf_op | source)
XLA Modules:
  0.0 86.3 jit_solution(11976505910348191487)
XLA Ops:
  0.0 84.6 %moe.1 = bf16[128,1280]{1,0:T(8,128)(2,1)} custom-call(bf16[128,1280]{1,0:T(8,128)(2,1)} %x_ref.1, s32[6,128]{1,0:T(8,128)} %bitcast.2, f32[6,128]{1,0:T(8,128)} %bitcast.3, bf16[20,1280,384]{2,1,0:T(8,128)(2,1)} %wg_ref.1, bf16[20,1280,384]{2,1,0:T(8,128)(2,1)} %wu_ref.1, bf16[20,384,1280]{2,1,0:T(8,128)(2,1)} %wd_ref.1), custom_call_target="tpu_custom_call" | custom-call | tf_op jit(solution)/shard_map/moe/pallas_call | solution.py:386
  84.6 1.7 %copy.8 = bf16[128,1280]{1,0:T(8,128)(2,1)} copy(bf16[128,1280]{1,0:T(8,128)(2,1)} %moe.1) | data formatting | bytes 655360

commit v5 on v4

--- a/solution.py
+++ b/solution.py
@@ -158,15 +158,15 @@
         cols_ref[pl.ds(d * tok, tok), :] = jnp.transpose(slot_t[:, d * tok:(d + 1) * tok])
 
     def selection(blk):
-        cols = cols_ref[pl.ds(blk * tok, tok), :]
+        cols = cols_ref[pl.ds(pl.multiple_of(blk * tok, tok), tok), :]
         lanes = lax.broadcasted_iota(jnp.int32, (tok, rows), 1).astype(F32)
         hit = cols[:, 0:1] == lanes
         for j in range(1, top_k):
             hit = hit | (cols[:, j:j + 1] == lanes)
         return jnp.where(hit, 1.0, 0.0).astype(BF16)
 
-    qp_ref[...] = selection(ORDER.index(YP))
-    qn_ref[...] = selection(ORDER.index(YN))
+    qp_ref[...] = selection(ORDER.index(DP))
+    qn_ref[...] = selection(ORDER.index(DG))
 
     def forward(at, part, hops):
         for to in hops:
@@ -298,62 +298,70 @@
             src_ref=c_ref.at[2 * h + 1], dst_ref=d_ref.at[h], send_sem=ds_sem.at[h], recv_sem=dr_sem.at[h],
             device_id=dev(PC), device_id_type=pl.DeviceIdType.MESH)
 
-    def combine_loop(count, pick):
-        def body(i, carry):
-            blk = pick(i)
-            q_ref[...] = selection(pl.multiple_of(blk, 1))
-            combine(q_ref, blk, range(d_model // step))
-
-            @pl.when(blk % 2 == 1)
-            def _():
-                swap_copy(blk // 2).start()
-            return carry
-
-        lax.fori_loop(0, count, body, 0)
-
     everything = pl.ds(0, d_model)
 
     def split_rows(h, at):
-        cols = cols_ref[pl.ds(2 * h * tok, tok), :]
+        cols = cols_ref[pl.ds(pl.multiple_of(2 * h * tok, tok), tok), :]
         mine = c_ref[2 * h, :, at]
         other = d_ref[h, :, at]
         c_ref[2 * h, :, at] = jnp.where(cols[:, 6:7] > 0.5, mine, other)
         d_ref[h, :, at] = jnp.where(cols[:, 7:8] > 0.5, other, 0.0)
 
     def ship(i, src, dst, to):
-        return send(src, dst, ts_sem.at[i], tr_sem.at[i], to)
-
-    first_own = []
+        return Sent(src, dst, lambda: ts_sem.at[i], lambda: tr_sem.at[i], to)
+
+    first_far = []
+    hop = []
+    far = ORDER.index(DG)
     for i, chunks in enumerate((range(0, 2), range(2, d_model // step))):
         at = pl.ds(chunks[0] * step, len(chunks) * step)
-        combine(qp_ref, ORDER.index(YP), chunks)
-        swap = send(c_ref.at[ORDER.index(YP), :, at], d_ref.at[0, :, at], ns_sem.at[i], nr_sem.at[i], PC)
-        combine(qn_ref, ORDER.index(YN), chunks)
+        combine(qp_ref, far + 1, chunks)
+        swap = send(c_ref.at[far + 1, :, at], d_ref.at[far // 2, :, at], ns_sem.at[i, 0], nr_sem.at[i, 0], PC)
+        combine(qn_ref, far, chunks)
         swap.wait_recv()
-        split_rows(0, at)
-        first_own.append(send(c_ref.at[0, :, at], rf_ref.at[0, :, at], ns_sem.at[2 + i], nr_sem.at[2 + i], YN))
-    combine_loop(2, lambda i: 7 - i)
-    swap_copy(3).wait_recv()
-    split_rows(3, everything)
-    first_far = ship(1, c_ref.at[6], rf_ref.at[1], YN)
-    hop = ship(2, d_ref.at[3], rs_ref.at[0], XN)
-    combine_loop(4, lambda i: 3 + 2 * i - (i // 2) * 5)
-    hop.wait_recv()
+        split_rows(far // 2, at)
+        first_far.append(send(c_ref.at[far, :, at], rf_ref.at[1, :, at], ns_sem.at[i, 1], nr_sem.at[i, 1], YN))
+        hop.append(send(d_ref.at[far // 2, :, at], rs_ref.at[0, :, at], ns_sem.at[i, 2], nr_sem.at[i, 2], XN))
+
+    shipped = {}
+
+    def others(i, carry):
+        blk = i + 1 - 2 * (i % 2)
+        q_ref[...] = selection(blk)
+        combine(q_ref, blk, range(d_model // step))
+
+        @pl.when(i % 2 == 0)
+        def _():
+            swap_copy(i // 2).start()
+
+        @pl.when(i % 2 == 1)
+        def _():
+            swap_copy(i // 2).wait_recv()
+            split_rows(i // 2, everything)
+
+        @pl.when(i == 1)
+        def _():
+            shipped["first_own"] = ship(0, lambda: c_ref.at[0], lambda: rf_ref.at[0], YN)
+
+        @pl.when(i == 3)
+        def _():
+            shipped["far_second"] = ship(4, lambda: d_ref.at[1], lambda: rs_ref.at[2], XN)
+        return carry
+
+    lax.fori_loop(0, n_dev - 2, others, 0)
+
+    for copy in first_far:
+        copy.wait_recv()
+    gp_ref[...] = (c_ref[2] + rf_ref[1]).astype(BF16)
+    far_first = ship(5, lambda: gp_ref, lambda: gx_ref, XN)
+    for copy in hop:
+        copy.wait_recv()
     d_ref[0] = d_ref[0] + rs_ref[0]
-    second = ship(3, d_ref.at[0], rs_ref.at[1], YN)
-    for h in (1, 2):
-        swap_copy(h).wait_recv()
-        split_rows(h, everything)
-        if h == 1:
-            far_second = ship(4, d_ref.at[1], rs_ref.at[2], XN)
-
-    for copy in first_own:
-        copy.wait_recv()
+    second = ship(3, lambda: d_ref.at[0], lambda: rs_ref.at[1], YN)
+
+    shipped["first_own"].wait_recv()
     c_ref[4] = (c_ref[4] + rf_ref[0]).astype(BF16).astype(F32)
-    first_far.wait_recv()
-    gp_ref[...] = (c_ref[2] + rf_ref[1]).astype(BF16)
-    far_first = ship(5, gp_ref, gx_ref, XN)
-    far_second.wait_recv()
+    shipped["far_second"].wait_recv()
     d_ref[2] = d_ref[2] + rs_ref[2]
     far_first.wait_recv()
     c_ref[4] = c_ref[4] + gx_ref[...].astype(F32)
@@ -361,7 +369,7 @@
     y_ref[...] = (c_ref[4] + (d_ref[2] + rs_ref[1]).astype(BF16).astype(F32)).astype(BF16)
     for copy in pending:
         copy.wait_send()
-    for h in range(1, n_dev // 2):
+    for h in range(n_dev // 2 - 1):
         swap_copy(h).wait_send()
 
 
@@ -421,8 +429,8 @@
                 dma((n_dev // 2,)),
                 dma((6,)),
                 dma((6,)),
-                dma((4,)),
-                dma((4,)),
+                dma((2, 3)),
+                dma((2, 3)),
             ],
             compiler_params=pltpu.CompilerParams(
                 collective_id=0, has_side_effects=True, vmem_limit_bytes=67043328),

time: 86.5 us -> 83.5 us (0.965)
  Pallas kernels: 84.6 us -> 81.7 us
    pallas_call x1, Pallas kernels: 84.6 us -> 81.7 us  [device_step(): pl.pallas_call(functools.partial(moe_kernel, dims), out_shape=jax.ShapeDt...]
where the time goes in v5:
time: 83.5 us; the launch traced here: 83.4 us
  Pallas kernels  81.7 us (98%)
  local copies, waits for them, and re-layouts  1.72 us (2%)
    pallas_call x1, Pallas kernels, device_step(): pl.pallas_call(functools.partial(moe_kernel, dims), out_shape=jax.ShapeDt...  81.7 us
    unnamed x1, local copies, waits for them, and re-layouts  1.72 us

profile of v5, /device:TPU:0, one launch (start us, length us, event | category | flops | bytes accessed | tf_op | source)
XLA Modules:
  0.0 83.4 jit_solution(12534673424180129291)
XLA Ops:
  0.0 81.7 %moe.1 = bf16[128,1280]{1,0:T(8,128)(2,1)} custom-call(bf16[128,1280]{1,0:T(8,128)(2,1)} %x_ref.1, s32[6,128]{1,0:T(8,128)} %bitcast.2, f32[6,128]{1,0:T(8,128)} %bitcast.3, bf16[20,1280,384]{2,1,0:T(8,128)(2,1)} %wg_ref.1, bf16[20,1280,384]{2,1,0:T(8,128)(2,1)} %wu_ref.1, bf16[20,384,1280]{2,1,0:T(8,128)(2,1)} %wd_ref.1), custom_call_target="tpu_custom_call" | custom-call | tf_op jit(solution)/shard_map/moe/pallas_call | solution.py:394
  81.7 1.7 %copy.8 = bf16[128,1280]{1,0:T(8,128)(2,1)} copy(bf16[128,1280]{1,0:T(8,128)(2,1)} %moe.1) | data formatting | bytes 655360

commit v6 on v5

--- a/solution.py
+++ b/solution.py
@@ -11,6 +11,7 @@
 BF16 = jnp.bfloat16
 PACK = 5
 PAIR = 2
+PARTS = [(0,), (1, 2), (3, 4)]
 
 
 YN, YP, DG, DP = (0, 0, 1), (0, 1, 1), (1, 0, 1), (1, 1, 1)
@@ -23,10 +24,10 @@
 
 
 def moe_kernel(dims, x_ref, ids_ref, gates_ref, wg_ref, wu_ref, wd_ref, y_ref,
-               x_all, ids_all, gates_all, pos_ref, ge_ref, cols_ref, gate_ref, oh_ref, packed, hid_ref, osp, q_ref, qp_ref, qn_ref,
+               x_all, ids_own, gates_own, meta_all, pos_ref, ge_ref, cols_ref, gate_ref, oh_ref, packed, hid_ref, osp, qp_ref, qn_ref,
                c_ref, d_ref, rf_ref, rs_ref, gp_ref, gx_ref, wgu, wdn,
-               in_sem, w_sem, xs_sem, xr_sem, ms_sem, mr_sem, ds_sem, dr_sem, ts_sem, tr_sem, ns_sem, nr_sem):
-    n_loc, n_grp, n_exp, cap, top_k, n_slot = dims
+               in_sem, w_sem, o_sem, xs_sem, xr_sem, ms_sem, mr_sem, ds_sem, dr_sem, ts_sem, tr_sem, ns_sem, nr_sem):
+    n_loc, n_grp, n_exp, cap, top_k, n_in, n_out = dims
     tok, d_model = x_ref.shape
     half = tok // 2
     own = ORDER.index(ME)
@@ -42,24 +43,29 @@
         fx, fc, fl = to
         return {"grp": ((gx + fx) % 2) * 2 + (gc + fc) % 2, "loc": (l + fl) % 2}
 
-    def in_copies(e, slot):
+    def in_copies(e):
+        slot = e % n_in
         return (
             pltpu.make_async_copy(wg_ref.at[e], wgu.at[slot, :, pl.ds(0, ff)], w_sem.at[slot, 0]),
             pltpu.make_async_copy(wu_ref.at[e], wgu.at[slot, :, pl.ds(ff, ff)], w_sem.at[slot, 1]),
         )
 
-    def out_copy(e, slot):
-        return pltpu.make_async_copy(wd_ref.at[e], wdn.at[slot], w_sem.at[slot, 2])
+    def out_copy(e):
+        slot = e % n_out
+        return pltpu.make_async_copy(wd_ref.at[e], wdn.at[slot], o_sem.at[slot])
 
     def start_weights(e, carry):
-        for copy in in_copies(e, e):
+        for copy in in_copies(e):
             copy.start()
-        out_copy(e, e).start()
+
+        @pl.when(e < n_out)
+        def _():
+            out_copy(e).start()
         return carry
 
     loads = [
         pltpu.make_async_copy(src, dst, in_sem.at[i]) for i, (src, dst) in enumerate((
-            (x_ref, x_all.at[pl.ds(own * tok, tok), :]), (ids_ref, ids_all.at[own]), (gates_ref, gates_all.at[own])))]
+            (x_ref, x_all.at[pl.ds(own * tok, tok), :]), (ids_ref, ids_own), (gates_ref, gates_own)))]
     for copy in loads:
         copy.start()
 
@@ -67,10 +73,13 @@
     barrier = pltpu.get_barrier_semaphore()
     for r in peers:
         pl.semaphore_signal(barrier, inc=1, device_id=dev(r), device_id_type=pl.DeviceIdType.MESH)
-    lax.fori_loop(0, n_slot, start_weights, 0)
-    pl.semaphore_wait(barrier, len(peers))
+    lax.fori_loop(0, n_in, start_weights, 0)
     for copy in loads:
         copy.wait()
+    meta_all[own] = jnp.zeros_like(meta_all[own])
+    meta_all[own, 0:top_k, :] = ids_own[...].astype(F32)
+    meta_all[own, 8:8 + top_k, :] = gates_own[...]
+    pl.semaphore_wait(barrier, len(peers))
 
     pending = []
 
@@ -95,11 +104,6 @@
     def send(src, dst, s_sem, r_sem, to):
         return Sent(lambda: src, lambda: dst, lambda: s_sem, lambda: r_sem, to)
 
-    metas = []
-    for i, r in enumerate(peers):
-        for k, (src, dst) in enumerate(((ids_all.at[own], ids_all), (gates_all.at[own], gates_all))):
-            metas.append(send(src, dst.at[ORDER.index(r)], ms_sem.at[i, k], mr_sem.at[i, k], r))
-
     def x_rows(at, part):
         return x_all.at[pl.ds(ORDER.index(at) * tok + part * half, half), :]
 
@@ -110,14 +114,18 @@
         got[at, part] = Sent(lambda: x_rows(*src), lambda: x_rows(at, part), lambda: xs_sem.at[i],
                              lambda: xr_sem.at[ORDER.index(at) * 2 + part], to)
 
-    for part, to in ((0, XN), (1, YN), (1, XN), (0, YN), (0, PC), (1, PC)):
+    send_x((ME, 0), 0, XN, XN)
+    send_x((ME, 1), 1, YN, YN)
+    metas = [send(meta_all.at[own], meta_all.at[ORDER.index(r)], ms_sem.at[i], mr_sem.at[i], r)
+             for i, r in enumerate(peers)]
+    for part, to in ((1, XN), (0, YN), (0, PC), (1, PC)):
         send_x((ME, part), part, to, to)
 
     for copy in metas:
         copy.wait_recv()
 
-    ids_t = jnp.concatenate([ids_all[d] for d in range(n_dev)], axis=1).astype(F32)
-    gts_t = jnp.concatenate([gates_all[d] for d in range(n_dev)], axis=1)
+    ids_t = jnp.concatenate([meta_all[d, 0:8, :] for d in range(n_dev)], axis=1)
+    gts_t = jnp.concatenate([meta_all[d, 8:16, :] for d in range(n_dev)], axis=1)
     e_rows = 32
     e_iota = lax.broadcasted_iota(jnp.int32, (e_rows, n_tok), 0)
     e_ids = jnp.where(e_iota < n_exp, e_iota + (g * n_loc + l) * n_exp, -5).astype(F32)
@@ -227,17 +235,14 @@
     landed(DP, 1)
     pack(n_tok - 2 * tok, 2 * tok, True, None)
 
-    def ring(ref_copies, e):
-        return ref_copies(e, e % n_slot)
-
     def first_dot(e, i):
         at = pl.ds(pl.multiple_of(e * cap, 16), cap)
-        uv = jnp.dot(packed[at, :], wgu[e % n_slot], preferred_element_type=F32)
+        uv = jnp.dot(packed[at, :], wgu[e % n_in], preferred_element_type=F32)
         return (jax.nn.silu(uv[:, :ff]) * uv[:, ff:]).astype(BF16)
 
     def second_dot(hid, e):
         at = pl.ds(pl.multiple_of(e * cap, 16), cap)
-        out = jnp.dot(hid, wdn[e % n_slot], preferred_element_type=F32) * gate_ref[at, :]
+        out = jnp.dot(hid, wdn[e % n_out], preferred_element_type=F32) * gate_ref[at, :]
         hi = out.astype(BF16)
         rest = out - hi.astype(F32)
         mid = rest.astype(BF16)
@@ -246,7 +251,7 @@
         osp[2, at, :] = (rest - mid.astype(F32)).astype(BF16)
 
     def wait_in(e):
-        for copy in ring(in_copies, e):
+        for copy in in_copies(e):
             copy.wait()
 
     for i in range(PAIR):
@@ -258,53 +263,53 @@
         now = [p * PAIR + i for i in range(PAIR)]
         for e in now:
             wait_in(e + PAIR)
-            ring(out_copy, e).wait()
+            out_copy(e).wait()
         held = [hid_ref[i] for i in range(PAIR)]
         for i, e in enumerate(now):
+            second_dot(held[i], e)
             hid_ref[i] = first_dot(e + PAIR, i)
-            second_dot(held[i], e)
 
         for e in now:
-            @pl.when(e + PAIR + n_slot < n_exp)
+            @pl.when(e + PAIR + n_in < n_exp)
             def _():
-                for copy in in_copies(e + PAIR + n_slot, (e + PAIR) % n_slot):
+                for copy in in_copies(e + PAIR + n_in):
                     copy.start()
 
-            @pl.when(e + n_slot < n_exp)
+            @pl.when(e + n_out < n_exp)
             def _():
-                out_copy(e + n_slot, e % n_slot).start()
+                out_copy(e + n_out).start()
         return carry
 
     for i in range(PAIR):
-        if i + n_slot < n_exp:
-            for copy in in_copies(i + n_slot, i):
+        if i + n_in < n_exp:
+            for copy in in_copies(i + n_in):
                 copy.start()
     lax.fori_loop(0, n_exp // PAIR - 1, experts, 0)
     for i in range(PAIR):
-        ring(out_copy, n_exp - PAIR + i).wait()
+        out_copy(n_exp - PAIR + i).wait()
     for i in range(PAIR):
         second_dot(hid_ref[i], n_exp - PAIR + i)
 
-    def combine(q, blk, chunks):
+    def combine(q, buf, chunks):
         for n in chunks:
             at = pl.ds(n * step, step)
             total = jnp.dot(q[...], osp[0, :, at], preferred_element_type=F32)
             total += jnp.dot(q[...], osp[1, :, at], preferred_element_type=F32)
             total += jnp.dot(q[...], osp[2, :, at], preferred_element_type=F32)
-            c_ref[blk, :, at] = total
+            c_ref[buf, :, at] = total
 
     def swap_copy(h):
         return pltpu.make_async_remote_copy(
-            src_ref=c_ref.at[2 * h + 1], dst_ref=d_ref.at[h], send_sem=ds_sem.at[h], recv_sem=dr_sem.at[h],
+            src_ref=c_ref.at[n_dev // 2 + (h + 1) % 2], dst_ref=d_ref.at[h], send_sem=ds_sem.at[h], recv_sem=dr_sem.at[h],
             device_id=dev(PC), device_id_type=pl.DeviceIdType.MESH)
 
     everything = pl.ds(0, d_model)
 
     def split_rows(h, at):
         cols = cols_ref[pl.ds(pl.multiple_of(2 * h * tok, tok), tok), :]
-        mine = c_ref[2 * h, :, at]
+        mine = c_ref[h, :, at]
         other = d_ref[h, :, at]
-        c_ref[2 * h, :, at] = jnp.where(cols[:, 6:7] > 0.5, mine, other)
+        c_ref[h, :, at] = jnp.where(cols[:, 6:7] > 0.5, mine, other)
         d_ref[h, :, at] = jnp.where(cols[:, 7:8] > 0.5, other, 0.0)
 
     def ship(i, src, dst, to):
@@ -312,32 +317,41 @@
 
     first_far = []
     hop = []
-    far = ORDER.index(DG)
-    for i, chunks in enumerate((range(0, 2), range(2, d_model // step))):
+    far = ORDER.index(DG) // 2
+    swaps = []
+    for i, chunks in enumerate(PARTS):
         at = pl.ds(chunks[0] * step, len(chunks) * step)
-        combine(qp_ref, far + 1, chunks)
-        swap = send(c_ref.at[far + 1, :, at], d_ref.at[far // 2, :, at], ns_sem.at[i, 0], nr_sem.at[i, 0], PC)
+        combine(qp_ref, n_dev // 2, chunks)
+        swaps.append(send(c_ref.at[n_dev // 2, :, at], d_ref.at[far, :, at], ns_sem.at[i, 0], nr_sem.at[i, 0], PC))
         combine(qn_ref, far, chunks)
-        swap.wait_recv()
-        split_rows(far // 2, at)
+        swaps[i].wait_recv()
+        split_rows(far, at)
         first_far.append(send(c_ref.at[far, :, at], rf_ref.at[1, :, at], ns_sem.at[i, 1], nr_sem.at[i, 1], YN))
-        hop.append(send(d_ref.at[far // 2, :, at], rs_ref.at[0, :, at], ns_sem.at[i, 2], nr_sem.at[i, 2], XN))
+        hop.append(send(d_ref.at[far, :, at], rs_ref.at[0, :, at], ns_sem.at[i, 2], nr_sem.at[i, 2], XN))
+    for copy in swaps:
+        copy.wait_send()
+        pending.remove(copy)
 
     shipped = {}
 
     def others(i, carry):
-        blk = i + 1 - 2 * (i % 2)
-        q_ref[...] = selection(blk)
-        combine(q_ref, blk, range(d_model // step))
+        h = i // 2
+
+        @pl.when(i == 4)
+        def _():
+            swap_copy(0).wait_send()
+
+        qp_ref[...] = selection(i + 1 - 2 * (i % 2))
+        combine(qp_ref, (i % 2) * h + (1 - i % 2) * (n_dev // 2 + (h + 1) % 2), range(d_model // step))
 
         @pl.when(i % 2 == 0)
         def _():
-            swap_copy(i // 2).start()
+            swap_copy(h).start()
 
         @pl.when(i % 2 == 1)
         def _():
-            swap_copy(i // 2).wait_recv()
-            split_rows(i // 2, everything)
+            swap_copy(h).wait_recv()
+            split_rows(h, everything)
 
         @pl.when(i == 1)
         def _():
@@ -352,7 +366,7 @@
 
     for copy in first_far:
         copy.wait_recv()
-    gp_ref[...] = (c_ref[2] + rf_ref[1]).astype(BF16)
+    gp_ref[...] = (c_ref[1] + rf_ref[1]).astype(BF16)
     far_first = ship(5, lambda: gp_ref, lambda: gx_ref, XN)
     for copy in hop:
         copy.wait_recv()
@@ -360,16 +374,16 @@
     second = ship(3, lambda: d_ref.at[0], lambda: rs_ref.at[1], YN)
 
     shipped["first_own"].wait_recv()
-    c_ref[4] = (c_ref[4] + rf_ref[0]).astype(BF16).astype(F32)
+    c_ref[2] = (c_ref[2] + rf_ref[0]).astype(BF16).astype(F32)
     shipped["far_second"].wait_recv()
     d_ref[2] = d_ref[2] + rs_ref[2]
     far_first.wait_recv()
-    c_ref[4] = c_ref[4] + gx_ref[...].astype(F32)
+    c_ref[2] = c_ref[2] + gx_ref[...].astype(F32)
     second.wait_recv()
-    y_ref[...] = (c_ref[4] + (d_ref[2] + rs_ref[1]).astype(BF16).astype(F32)).astype(BF16)
+    y_ref[...] = (c_ref[2] + (d_ref[2] + rs_ref[1]).astype(BF16).astype(F32)).astype(BF16)
     for copy in pending:
         copy.wait_send()
-    for h in range(n_dev // 2 - 1):
+    for h in range(1, n_dev // 2 - 1):
         swap_copy(h).wait_send()
 
 
@@ -387,10 +401,10 @@
         n_tok = tok * n_dev
         cap = 8 * (n_tok * top_k // (4 * n_exp * n_dev) + 1)
         rows = n_exp * cap
-        n_slot = 9
+        n_in, n_out = 11, 10
         vmem = pltpu.VMEM
         dma = pltpu.SemaphoreType.DMA
-        dims = (n_loc, n_grp, n_exp, cap, top_k, n_slot)
+        dims = (n_loc, n_grp, n_exp, cap, top_k, n_in, n_out)
         return pl.pallas_call(
             functools.partial(moe_kernel, dims),
             out_shape=jax.ShapeDtypeStruct((tok, d_model), BF16),
@@ -398,8 +412,9 @@
             out_specs=pl.BlockSpec(memory_space=vmem),
             scratch_shapes=[
                 vmem((n_tok, d_model), BF16),
-                vmem((n_dev, top_k, tok), jnp.int32),
-                vmem((n_dev, top_k, tok), F32),
+                vmem((top_k, tok), jnp.int32),
+                vmem((top_k, tok), F32),
+                vmem((n_dev, 16, tok), F32),
                 vmem((32, n_tok), F32),
                 vmem((32, n_tok), F32),
                 vmem((n_tok, 8), F32),
@@ -410,27 +425,27 @@
                 vmem((3, rows, d_model), BF16),
                 vmem((tok, rows), BF16),
                 vmem((tok, rows), BF16),
-                vmem((tok, rows), BF16),
-                vmem((n_dev, tok, d_model), F32),
+                vmem((n_dev // 2 + 2, tok, d_model), F32),
                 vmem((n_dev // 2, tok, d_model), F32),
                 vmem((2, tok, d_model), F32),
                 vmem((3, tok, d_model), F32),
                 vmem((tok, d_model), BF16),
                 vmem((tok, d_model), BF16),
-                vmem((n_slot, d_model, 2 * ff), BF16),
-                vmem((n_slot, ff, d_model), BF16),
+                vmem((n_in, d_model, 2 * ff), BF16),
+                vmem((n_out, ff, d_model), BF16),
                 dma((3,)),
-                dma((n_slot, 3)),
+                dma((n_in, 2)),
+                dma((n_out,)),
                 dma((14,)),
                 dma((16,)),
-                dma((7, 2)),
-                dma((7, 2)),
+                dma((7,)),
+                dma((7,)),
                 dma((n_dev // 2,)),
                 dma((n_dev // 2,)),
                 dma((6,)),
                 dma((6,)),
-                dma((2, 3)),
-                dma((2, 3)),
+                dma((3, 3)),
+                dma((3, 3)),
             ],
             compiler_params=pltpu.CompilerParams(
                 collective_id=0, has_side_effects=True, vmem_limit_bytes=67043328),

time: 83.5 us -> 84 us (level)
  no operation moved by 1% of the time
where the time goes in v6:
time: 84 us; the launch traced here: 83.9 us
  Pallas kernels  82.1 us (98%)
  local copies, waits for them, and re-layouts  1.72 us (2%)
    pallas_call x1, Pallas kernels, device_step(): pl.pallas_call(functools.partial(moe_kernel, dims), out_shape=jax.ShapeDt...  82.1 us
    unnamed x1, local copies, waits for them, and re-layouts  1.72 us

profile of v6, /device:TPU:0, one launch (start us, length us, event | category | flops | bytes accessed | tf_op | source)
XLA Modules:
  0.0 83.9 jit_solution(4924380700925634693)
XLA Ops:
  0.0 82.1 %moe.1 = bf16[128,1280]{1,0:T(8,128)(2,1)} custom-call(bf16[128,1280]{1,0:T(8,128)(2,1)} %x_ref.1, s32[6,128]{1,0:T(8,128)} %bitcast.2, f32[6,128]{1,0:T(8,128)} %bitcast.3, bf16[20,1280,384]{2,1,0:T(8,128)(2,1)} %wg_ref.1, bf16[20,1280,384]{2,1,0:T(8,128)(2,1)} %wu_ref.1, bf16[20,384,1280]{2,1,0:T(8,128)(2,1)} %wd_ref.1), custom_call_target="tpu_custom_call" | custom-call | tf_op jit(solution)/shard_map/moe/pallas_call | solution.py:408
  82.1 1.7 %copy.8 = bf16[128,1280]{1,0:T(8,128)(2,1)} copy(bf16[128,1280]{1,0:T(8,128)(2,1)} %moe.1) | data formatting | bytes 655360

commit v7 on v6

--- a/solution.py
+++ b/solution.py
@@ -120,6 +120,18 @@
              for i, r in enumerate(peers)]
     for part, to in ((1, XN), (0, YN), (0, PC), (1, PC)):
         send_x((ME, part), part, to, to)
+
+    def forward(at, part, hops):
+        for to in hops:
+            send_x((at, part), part, to, flip(at, to))
+
+    def landed(at, part):
+        got[at, part].wait_recv()
+
+    landed(XN, 0)
+    forward(XN, 0, [YN, PC])
+    landed(YN, 1)
+    forward(YN, 1, [XN, PC])
 
     for copy in metas:
         copy.wait_recv()
@@ -176,17 +188,6 @@
     qp_ref[...] = selection(ORDER.index(DP))
     qn_ref[...] = selection(ORDER.index(DG))
 
-    def forward(at, part, hops):
-        for to in hops:
-            send_x((at, part), part, to, flip(at, to))
-
-    def landed(at, part):
-        got[at, part].wait_recv()
-
-    landed(XN, 0)
-    forward(XN, 0, [YN, PC])
-    landed(YN, 1)
-    forward(YN, 1, [XN, PC])
     landed(XN, 1)
     forward(XN, 1, [PC])
     landed(YN, 0)

time: 84 us -> 82.8 us (0.986)
  Pallas kernels: 82.1 us -> 81 us
    pallas_call x1, Pallas kernels: 82.1 us -> 81 us  [device_step(): pl.pallas_call(functools.partial(moe_kernel, dims), out_shape=jax.ShapeDt...]
where the time goes in v7:
time: 82.8 us; the launch traced here: 82.7 us
  Pallas kernels  81 us (98%)
  local copies, waits for them, and re-layouts  1.72 us (2%)
    pallas_call x1, Pallas kernels, device_step(): pl.pallas_call(functools.partial(moe_kernel, dims), out_shape=jax.ShapeDt...  81 us
    unnamed x1, local copies, waits for them, and re-layouts  1.72 us

profile of v7, /device:TPU:0, one launch (start us, length us, event | category | flops | bytes accessed | tf_op | source)
XLA Modules:
  0.0 82.7 jit_solution(311828363643742713)
XLA Ops:
  0.0 81.0 %moe.1 = bf16[128,1280]{1,0:T(8,128)(2,1)} custom-call(bf16[128,1280]{1,0:T(8,128)(2,1)} %x_ref.1, s32[6,128]{1,0:T(8,128)} %bitcast.2, f32[6,128]{1,0:T(8,128)} %bitcast.3, bf16[20,1280,384]{2,1,0:T(8,128)(2,1)} %wg_ref.1, bf16[20,1280,384]{2,1,0:T(8,128)(2,1)} %wu_ref.1, bf16[20,384,1280]{2,1,0:T(8,128)(2,1)} %wd_ref.1), custom_call_target="tpu_custom_call" | custom-call | tf_op jit(solution)/shard_map/moe/pallas_call | solution.py:409
  81.0 1.7 %copy.8 = bf16[128,1280]{1,0:T(8,128)(2,1)} copy(bf16[128,1280]{1,0:T(8,128)(2,1)} %moe.1) | data formatting | bytes 655360

commit v8 on v7

--- a/solution.py
+++ b/solution.py
@@ -10,7 +10,7 @@
 F32 = jnp.float32
 BF16 = jnp.bfloat16
 PACK = 5
-PAIR = 2
+PAIR = 4
 PARTS = [(0,), (1, 2), (3, 4)]
 
 
@@ -188,13 +188,6 @@
     qp_ref[...] = selection(ORDER.index(DP))
     qn_ref[...] = selection(ORDER.index(DG))
 
-    landed(XN, 1)
-    forward(XN, 1, [PC])
-    landed(YN, 0)
-    forward(YN, 0, [PC])
-    landed(YP, 0)
-    landed(YP, 1)
-
     step = 256
 
     def pack(first, count, add, midway):
@@ -223,15 +216,25 @@
 
         lax.fori_loop(0, n_exp // PACK, body, 0)
 
+    def early():
+        landed(XN, 1)
+        forward(XN, 1, [PC])
+        landed(YN, 0)
+        forward(YN, 0, [PC])
+
     def diagonal():
         for part in (0, 1):
             landed(DG, part)
             forward(DG, part, [PC])
 
-    for at in (XP, PC):
-        landed(at, 0)
-        landed(at, 1)
-    pack(0, n_tok - 2 * tok, False, diagonal)
+    landed(PC, 0)
+    landed(PC, 1)
+    pack(4 * tok, 2 * tok, False, early)
+    landed(YP, 0)
+    landed(YP, 1)
+    landed(XP, 0)
+    landed(XP, 1)
+    pack(0, 4 * tok, True, diagonal)
     landed(DP, 0)
     landed(DP, 1)
     pack(n_tok - 2 * tok, 2 * tok, True, None)

time: 82.8 us -> 82.8 us (level)
  no operation moved by 1% of the time
where the time goes in v8:
time: 82.8 us; the launch traced here: 82.7 us
  Pallas kernels  80.9 us (98%)
  local copies, waits for them, and re-layouts  1.72 us (2%)
    pallas_call x1, Pallas kernels, device_step(): pl.pallas_call(functools.partial(moe_kernel, dims), out_shape=jax.ShapeDt...  80.9 us
    unnamed x1, local copies, waits for them, and re-layouts  1.72 us

profile of v8, /device:TPU:0, one launch (start us, length us, event | category | flops | bytes accessed | tf_op | source)
XLA Modules:
  0.0 82.7 jit_solution(4298442992224831968)
XLA Ops:
  0.0 80.9 %moe.1 = bf16[128,1280]{1,0:T(8,128)(2,1)} custom-call(bf16[128,1280]{1,0:T(8,128)(2,1)} %x_ref.1, s32[6,128]{1,0:T(8,128)} %bitcast.2, f32[6,128]{1,0:T(8,128)} %bitcast.3, bf16[20,1280,384]{2,1,0:T(8,128)(2,1)} %wg_ref.1, bf16[20,1280,384]{2,1,0:T(8,128)(2,1)} %wu_ref.1, bf16[20,384,1280]{2,1,0:T(8,128)(2,1)} %wd_ref.1), custom_call_target="tpu_custom_call" | custom-call | tf_op jit(solution)/shard_map/moe/pallas_call | solution.py:412
  81.0 1.7 %copy.8 = bf16[128,1280]{1,0:T(8,128)(2,1)} copy(bf16[128,1280]{1,0:T(8,128)(2,1)} %moe.1) | data formatting | bytes 655360

commit v9 on v8

--- a/solution.py
+++ b/solution.py
@@ -10,7 +10,7 @@
 F32 = jnp.float32
 BF16 = jnp.bfloat16
 PACK = 5
-PAIR = 4
+PAIR = 2
 PARTS = [(0,), (1, 2), (3, 4)]
 
 

time: 82.8 us -> 82.3 us (level)
  no operation moved by 1% of the time
where the time goes in v9:
time: 82.3 us; the launch traced here: 82.1 us
  Pallas kernels  80.4 us (98%)
  local copies, waits for them, and re-layouts  1.72 us (2%)
    pallas_call x1, Pallas kernels, device_step(): pl.pallas_call(functools.partial(moe_kernel, dims), out_shape=jax.ShapeDt...  80.4 us
    unnamed x1, local copies, waits for them, and re-layouts  1.72 us

profile of v9, /device:TPU:0, one launch (start us, length us, event | category | flops | bytes accessed | tf_op | source)
XLA Modules:
  0.0 82.1 jit_solution(16537328533287621132)
XLA Ops:
  0.0 80.4 %moe.1 = bf16[128,1280]{1,0:T(8,128)(2,1)} custom-call(bf16[128,1280]{1,0:T(8,128)(2,1)} %x_ref.1, s32[6,128]{1,0:T(8,128)} %bitcast.2, f32[6,128]{1,0:T(8,128)} %bitcast.3, bf16[20,1280,384]{2,1,0:T(8,128)(2,1)} %wg_ref.1, bf16[20,1280,384]{2,1,0:T(8,128)(2,1)} %wu_ref.1, bf16[20,384,1280]{2,1,0:T(8,128)(2,1)} %wd_ref.1), custom_call_target="tpu_custom_call" | custom-call | tf_op jit(solution)/shard_map/moe/pallas_call | solution.py:412
  80.4 1.7 %copy.8 = bf16[128,1280]{1,0:T(8,128)(2,1)} copy(bf16[128,1280]{1,0:T(8,128)(2,1)} %moe.1) | data formatting | bytes 655360

commit v10 on v9

--- a/solution.py
+++ b/solution.py
@@ -237,7 +237,23 @@
     pack(0, 4 * tok, True, diagonal)
     landed(DP, 0)
     landed(DP, 1)
-    pack(n_tok - 2 * tok, 2 * tok, True, None)
+
+    def pack_late(e, count):
+        toks = pl.ds(n_tok - 2 * tok, 2 * tok)
+        picks = []
+        for i in range(count):
+            where = lax.broadcasted_iota(jnp.int32, (cap, 2 * tok), 0).astype(F32) == pos_ref[pl.ds(e + i, 1), toks]
+            picks.append(jnp.where(where, 1.0, 0.0).astype(BF16))
+            at = pl.ds(pl.multiple_of((e + i) * cap, 16), cap)
+            gate_ref[at, :] += jnp.sum(jnp.where(where, ge_ref[pl.ds(e + i, 1), toks], 0.0), axis=1, keepdims=True)
+        pick = jnp.concatenate(picks, axis=0)
+        at = pl.ds(pl.multiple_of(e * cap, 16), count * cap)
+        for n in range(d_model // step):
+            cols = pl.ds(n * step, step)
+            part = jnp.dot(pick, x_all[toks, cols], preferred_element_type=F32)
+            packed[at, cols] = (part + packed[at, cols].astype(F32)).astype(BF16)
+
+    pack_late(0, 2 * PAIR)
 
     def first_dot(e, i):
         at = pl.ds(pl.multiple_of(e * cap, 16), cap)
@@ -263,7 +279,7 @@
     for i in range(PAIR):
         hid_ref[i] = first_dot(i, i)
 
-    def experts(p, carry):
+    def experts(p, late):
         now = [p * PAIR + i for i in range(PAIR)]
         for e in now:
             wait_in(e + PAIR)
@@ -272,6 +288,8 @@
         for i, e in enumerate(now):
             second_dot(held[i], e)
             hid_ref[i] = first_dot(e + PAIR, i)
+        if late:
+            pack_late((p + 2) * PAIR, PAIR)
 
         for e in now:
             @pl.when(e + PAIR + n_in < n_exp)
@@ -282,13 +300,17 @@
             @pl.when(e + n_out < n_exp)
             def _():
                 out_copy(e + n_out).start()
-        return carry
 
     for i in range(PAIR):
         if i + n_in < n_exp:
             for copy in in_copies(i + n_in):
                 copy.start()
-    lax.fori_loop(0, n_exp // PAIR - 1, experts, 0)
+    def turn(p, carry):
+        experts(p, True)
+        return carry
+
+    lax.fori_loop(0, n_exp // PAIR - 2, turn, 0)
+    experts(n_exp // PAIR - 2, False)
     for i in range(PAIR):
         out_copy(n_exp - PAIR + i).wait()
     for i in range(PAIR):

time: 82.3 us -> 81.3 us (0.988)
  Pallas kernels: 80.4 us -> 79.5 us
    pallas_call x1, Pallas kernels: 80.4 us -> 79.5 us  [device_step(): pl.pallas_call(functools.partial(moe_kernel, dims), out_shape=jax.ShapeDt...]
where the time goes in v10:
time: 81.3 us; the launch traced here: 81.2 us
  Pallas kernels  79.5 us (98%)
  local copies, waits for them, and re-layouts  1.72 us (2%)
    pallas_call x1, Pallas kernels, device_step(): pl.pallas_call(functools.partial(moe_kernel, dims), out_shape=jax.ShapeDt...  79.5 us
    unnamed x1, local copies, waits for them, and re-layouts  1.72 us

profile of v10, /device:TPU:0, one launch (start us, length us, event | category | flops | bytes accessed | tf_op | source)
XLA Modules:
  0.0 81.2 jit_solution(148297459956212147)
XLA Ops:
  0.0 79.5 %moe.1 = bf16[128,1280]{1,0:T(8,128)(2,1)} custom-call(bf16[128,1280]{1,0:T(8,128)(2,1)} %x_ref.1, s32[6,128]{1,0:T(8,128)} %bitcast.2, f32[6,128]{1,0:T(8,128)} %bitcast.3, bf16[20,1280,384]{2,1,0:T(8,128)(2,1)} %wg_ref.1, bf16[20,1280,384]{2,1,0:T(8,128)(2,1)} %wu_ref.1, bf16[20,384,1280]{2,1,0:T(8,128)(2,1)} %wd_ref.1), custom_call_target="tpu_custom_call" | custom-call | tf_op jit(solution)/shard_map/moe/pallas_call | solution.py:434
  79.5 1.7 %copy.8 = bf16[128,1280]{1,0:T(8,128)(2,1)} copy(bf16[128,1280]{1,0:T(8,128)(2,1)} %moe.1) | data formatting | bytes 655360

commit v11 on v10

--- a/solution.py
+++ b/solution.py
@@ -186,11 +186,10 @@
         return jnp.where(hit, 1.0, 0.0).astype(BF16)
 
     qp_ref[...] = selection(ORDER.index(DP))
-    qn_ref[...] = selection(ORDER.index(DG))
 
     step = 256
 
-    def pack(first, count, add, midway):
+    def pack(first, count, add, midway, turn):
         toks = pl.ds(first, count)
 
         def body(p, carry):
@@ -209,7 +208,7 @@
                     part = part + packed[at, cols].astype(F32)
                 packed[at, cols] = part.astype(BF16)
             if midway is not None:
-                @pl.when(p == 1)
+                @pl.when(p == turn)
                 def _():
                     midway()
             return carry
@@ -229,12 +228,12 @@
 
     landed(PC, 0)
     landed(PC, 1)
-    pack(4 * tok, 2 * tok, False, early)
+    pack(4 * tok, 2 * tok, False, early, 0)
     landed(YP, 0)
     landed(YP, 1)
     landed(XP, 0)
     landed(XP, 1)
-    pack(0, 4 * tok, True, diagonal)
+    pack(0, 4 * tok, True, diagonal, 1)
     landed(DP, 0)
     landed(DP, 1)
 
@@ -349,6 +348,8 @@
         at = pl.ds(chunks[0] * step, len(chunks) * step)
         combine(qp_ref, n_dev // 2, chunks)
         swaps.append(send(c_ref.at[n_dev // 2, :, at], d_ref.at[far, :, at], ns_sem.at[i, 0], nr_sem.at[i, 0], PC))
+        if i == 0:
+            qn_ref[...] = selection(ORDER.index(DG))
         combine(qn_ref, far, chunks)
         swaps[i].wait_recv()
         split_rows(far, at)

time: 81.3 us -> 81.4 us (level)
  no operation moved by 1% of the time
where the time goes in v11:
time: 81.4 us; the launch traced here: 81.3 us
  Pallas kernels  79.6 us (98%)
  local copies, waits for them, and re-layouts  1.72 us (2%)
    pallas_call x1, Pallas kernels, device_step(): pl.pallas_call(functools.partial(moe_kernel, dims), out_shape=jax.ShapeDt...  79.6 us
    unnamed x1, local copies, waits for them, and re-layouts  1.72 us

profile of v11, /device:TPU:0, one launch (start us, length us, event | category | flops | bytes accessed | tf_op | source)
XLA Modules:
  0.0 81.3 jit_solution(14916374493833995081)
XLA Ops:
  0.0 79.6 %moe.1 = bf16[128,1280]{1,0:T(8,128)(2,1)} custom-call(bf16[128,1280]{1,0:T(8,128)(2,1)} %x_ref.1, s32[6,128]{1,0:T(8,128)} %bitcast.2, f32[6,128]{1,0:T(8,128)} %bitcast.3, bf16[20,1280,384]{2,1,0:T(8,128)(2,1)} %wg_ref.1, bf16[20,1280,384]{2,1,0:T(8,128)(2,1)} %wu_ref.1, bf16[20,384,1280]{2,1,0:T(8,128)(2,1)} %wd_ref.1), custom_call_target="tpu_custom_call" | custom-call | tf_op jit(solution)/shard_map/moe/pallas_call | solution.py:435
  79.6 1.7 %copy.8 = bf16[128,1280]{1,0:T(8,128)(2,1)} copy(bf16[128,1280]{1,0:T(8,128)(2,1)} %moe.1) | data formatting | bytes 655360

commit v12 on v11

--- a/solution.py
+++ b/solution.py
@@ -228,7 +228,7 @@
 
     landed(PC, 0)
     landed(PC, 1)
-    pack(4 * tok, 2 * tok, False, early, 0)
+    pack(4 * tok, 2 * tok, False, early, 1)
     landed(YP, 0)
     landed(YP, 1)
     landed(XP, 0)

time: 81.4 us -> 81.4 us (level)
  no operation moved by 1% of the time
where the time goes in v12:
time: 81.4 us; the launch traced here: 81.3 us
  Pallas kernels  79.6 us (98%)
  local copies, waits for them, and re-layouts  1.72 us (2%)
    pallas_call x1, Pallas kernels, device_step(): pl.pallas_call(functools.partial(moe_kernel, dims), out_shape=jax.ShapeDt...  79.6 us
    unnamed x1, local copies, waits for them, and re-layouts  1.72 us

profile of v12, /device:TPU:0, one launch (start us, length us, event | category | flops | bytes accessed | tf_op | source)
XLA Modules:
  0.0 81.3 jit_solution(14634686936455696056)
XLA Ops:
  0.0 79.6 %moe.1 = bf16[128,1280]{1,0:T(8,128)(2,1)} custom-call(bf16[128,1280]{1,0:T(8,128)(2,1)} %x_ref.1, s32[6,128]{1,0:T(8,128)} %bitcast.2, f32[6,128]{1,0:T(8,128)} %bitcast.3, bf16[20,1280,384]{2,1,0:T(8,128)(2,1)} %wg_ref.1, bf16[20,1280,384]{2,1,0:T(8,128)(2,1)} %wu_ref.1, bf16[20,384,1280]{2,1,0:T(8,128)(2,1)} %wd_ref.1), custom_call_target="tpu_custom_call" | custom-call | tf_op jit(solution)/shard_map/moe/pallas_call | solution.py:435
  79.6 1.7 %copy.8 = bf16[128,1280]{1,0:T(8,128)(2,1)} copy(bf16[128,1280]{1,0:T(8,128)(2,1)} %moe.1) | data formatting | bytes 655360

commit v13 on v11

--- a/solution.py
+++ b/solution.py
@@ -186,6 +186,7 @@
         return jnp.where(hit, 1.0, 0.0).astype(BF16)
 
     qp_ref[...] = selection(ORDER.index(DP))
+    qn_ref[...] = selection(ORDER.index(DG))
 
     step = 256
 
@@ -233,7 +234,7 @@
     landed(YP, 1)
     landed(XP, 0)
     landed(XP, 1)
-    pack(0, 4 * tok, True, diagonal, 1)
+    pack(0, 4 * tok, True, diagonal, 0)
     landed(DP, 0)
     landed(DP, 1)
 
@@ -348,8 +349,6 @@
         at = pl.ds(chunks[0] * step, len(chunks) * step)
         combine(qp_ref, n_dev // 2, chunks)
         swaps.append(send(c_ref.at[n_dev // 2, :, at], d_ref.at[far, :, at], ns_sem.at[i, 0], nr_sem.at[i, 0], PC))
-        if i == 0:
-            qn_ref[...] = selection(ORDER.index(DG))
         combine(qn_ref, far, chunks)
         swaps[i].wait_recv()
         split_rows(far, at)

time: 81.4 us -> 82 us (level)
  no operation moved by 1% of the time
where the time goes in v13:
time: 82 us; the launch traced here: 81.9 us
  Pallas kernels  80.2 us (98%)
  local copies, waits for them, and re-layouts  1.72 us (2%)
    pallas_call x1, Pallas kernels, device_step(): pl.pallas_call(functools.partial(moe_kernel, dims), out_shape=jax.ShapeDt...  80.2 us
    unnamed x1, local copies, waits for them, and re-layouts  1.72 us

profile of v13, /device:TPU:0, one launch (start us, length us, event | category | flops | bytes accessed | tf_op | source)
XLA Modules:
  0.0 81.9 jit_solution(4352555501538220539)
XLA Ops:
  0.0 80.2 %moe.1 = bf16[128,1280]{1,0:T(8,128)(2,1)} custom-call(bf16[128,1280]{1,0:T(8,128)(2,1)} %x_ref.1, s32[6,128]{1,0:T(8,128)} %bitcast.2, f32[6,128]{1,0:T(8,128)} %bitcast.3, bf16[20,1280,384]{2,1,0:T(8,128)(2,1)} %wg_ref.1, bf16[20,1280,384]{2,1,0:T(8,128)(2,1)} %wu_ref.1, bf16[20,384,1280]{2,1,0:T(8,128)(2,1)} %wd_ref.1), custom_call_target="tpu_custom_call" | custom-call | tf_op jit(solution)/shard_map/moe/pallas_call | solution.py:434
  80.2 1.7 %copy.8 = bf16[128,1280]{1,0:T(8,128)(2,1)} copy(bf16[128,1280]{1,0:T(8,128)(2,1)} %moe.1) | data formatting | bytes 655360

commit v14 on v13

--- a/solution.py
+++ b/solution.py
@@ -229,12 +229,12 @@
 
     landed(PC, 0)
     landed(PC, 1)
-    pack(4 * tok, 2 * tok, False, early, 0)
+    pack(4 * tok, 2 * tok, False, early, 1)
     landed(YP, 0)
     landed(YP, 1)
     landed(XP, 0)
     landed(XP, 1)
-    pack(0, 4 * tok, True, diagonal, 0)
+    pack(0, 4 * tok, True, diagonal, 2)
     landed(DP, 0)
     landed(DP, 1)
 

time: 82 us -> 81.6 us (level)
  no operation moved by 1% of the time
where the time goes in v14:
time: 81.6 us; the launch traced here: 81.5 us
  Pallas kernels  79.8 us (98%)
  local copies, waits for them, and re-layouts  1.72 us (2%)
    pallas_call x1, Pallas kernels, device_step(): pl.pallas_call(functools.partial(moe_kernel, dims), out_shape=jax.ShapeDt...  79.8 us
    unnamed x1, local copies, waits for them, and re-layouts  1.72 us

profile of v14, /device:TPU:0, one launch (start us, length us, event | category | flops | bytes accessed | tf_op | source)
XLA Modules:
  0.0 81.5 jit_solution(8381438305339274095)
XLA Ops:
  0.0 79.8 %moe.1 = bf16[128,1280]{1,0:T(8,128)(2,1)} custom-call(bf16[128,1280]{1,0:T(8,128)(2,1)} %x_ref.1, s32[6,128]{1,0:T(8,128)} %bitcast.2, f32[6,128]{1,0:T(8,128)} %bitcast.3, bf16[20,1280,384]{2,1,0:T(8,128)(2,1)} %wg_ref.1, bf16[20,1280,384]{2,1,0:T(8,128)(2,1)} %wu_ref.1, bf16[20,384,1280]{2,1,0:T(8,128)(2,1)} %wd_ref.1), custom_call_target="tpu_custom_call" | custom-call | tf_op jit(solution)/shard_map/moe/pallas_call | solution.py:434
  79.8 1.7 %copy.8 = bf16[128,1280]{1,0:T(8,128)(2,1)} copy(bf16[128,1280]{1,0:T(8,128)(2,1)} %moe.1) | data formatting | bytes 655360
